TPU v7x, 32 devices: a whole 2x2x4 slice. The times are simulated.
32 devices in a mesh: dp: 8 (over z, x), mp: 4 (over y, core).
Axes of the slice: x: 2, y: 2, z: 4, core: 2. Of those that a mesh axis runs over, the one named last changes fastest.
Arguments:
- tokens: bfloat16 [16384, 1024], P('dp'), may hold values from -6 to 6
- cotangent: bfloat16 [16384, 1024], P('dp'), may hold values from -15 to 15
- item_lengths: int32 [8, 8], P('dp'), may hold values from 1 to 1024, 2048 in all within a row
- w_qkv: bfloat16 [3, 1024, 1024], P(None, None, 'mp'), may hold values from -0.1875 to 0.1875
- b_qv: float32 [2, 1024], P(None, 'mp'), may hold values from -3 to 3
- w_out: bfloat16 [1024, 1024], P('mp'), may hold values from -0.75 to 0.75
- b_out: float32 [1024], replicated, may hold values from -1.75 to 1.75
- w_fc1: bfloat16 [1024, 4096], P(None, 'mp'), may hold values from -0.1875 to 0.1875
- b_fc1: float32 [4096], P('mp'), may hold values from -3 to 3
- w_fc2: bfloat16 [4096, 1024], P('mp'), may hold values from -0.09375 to 0.09375
- b_fc2: float32 [1024], replicated, may hold values from -1.75 to 1.75
- ln1_gain: float32 [1024], replicated, may hold values from 0.5 to 1.5
- ln1_bias: float32 [1024], replicated, may hold values from -1.75 to 1.75
- ln2_gain: float32 [1024], replicated, may hold values from 0.5 to 1.5
- ln2_bias: float32 [1024], replicated, may hold values from -1.75 to 1.75
Outputs:
- output: bfloat16 [16384, 1024], P('dp')
- grad_tokens: float32 [16384, 1024], P('dp')
- grad_w_qkv: float32 [3, 1024, 1024], P(None, 'dp', 'mp')
- grad_b_qv: float32 [2, 1024], P(None, 'mp')
- grad_w_out: float32 [1024, 1024], P('mp', 'dp')
- grad_b_out: float32 [1024], replicated
- grad_w_fc1: float32 [1024, 4096], P('dp', 'mp')
- grad_b_fc1: float32 [4096], P('mp')
- grad_w_fc2: float32 [4096, 1024], P('mp', 'dp')
- grad_b_fc2: float32 [1024], replicated
- grad_ln1_gain: float32 [1024], replicated
- grad_ln1_bias: float32 [1024], replicated
- grad_ln2_gain: float32 [1024], replicated
- grad_ln2_bias: float32 [1024], replicated
Inputs may be any that keep to these rules, and one draw needn't show every extreme that they name: `item_lengths`: each row sums to 2048, and each row's longest item has exactly 1024 patches.
All inputs are finite; a program needn't handle non-finite values.
Results may differ from a plain program's by a relative error of at most 0.019.
Values may be sent and summed in bfloat16 or wider, within the bound.
A program may use at most 192 MiB of HBM per device.

v0:
```python
import jax
import jax.numpy as jnp
from jax import lax
from jax.sharding import PartitionSpec as P

HEAD = 64
QBLOCK = 512


def normalize(values, gain, shift):
    center = jnp.mean(values, axis=-1, keepdims=True)
    centered = values - center
    spread = jnp.mean(centered * centered, axis=-1, keepdims=True)
    return centered * lax.rsqrt(spread + 1e-06) * gain + shift


def exact_gelu(values):
    return jax.nn.gelu(values, approximate=False)


def segment_ids(lengths_row, row_count):
    ends = jnp.cumsum(lengths_row)
    positions = jnp.arange(row_count, dtype=jnp.int32)
    return jnp.sum((positions[:, None] >= ends[None, :]).astype(jnp.int32), axis=1)


def per_device(
    tokens,
    cotangent,
    item_lengths,
    w_qkv,
    b_qv,
    w_out,
    b_out,
    w_fc1,
    b_fc1,
    w_fc2,
    b_fc2,
    ln1_gain,
    ln1_bias,
    ln2_gain,
    ln2_bias,
):
    row_count = tokens.shape[0]
    local_cols = w_qkv.shape[2]
    heads_here = local_cols // HEAD
    blocks = row_count // QBLOCK
    score_scale = HEAD ** (-0.5)
    segments = segment_ids(item_lengths[0], row_count)
    seg_blocks = segments.reshape(blocks, QBLOCK)
    inputs = tokens.astype(jnp.float32)
    norm_one, norm_one_back = jax.vjp(normalize, inputs, ln1_gain, ln1_bias)
    normed_one = norm_one.astype(jnp.bfloat16)
    queries = (jnp.dot(normed_one, w_qkv[0], preferred_element_type=jnp.float32) + b_qv[0]).astype(
        jnp.bfloat16
    )
    key_rows = jnp.dot(normed_one, w_qkv[1], preferred_element_type=jnp.float32).astype(
        jnp.bfloat16
    )
    value_rows = (
        jnp.dot(normed_one, w_qkv[2], preferred_element_type=jnp.float32) + b_qv[1]
    ).astype(jnp.bfloat16)
    key_heads = key_rows.reshape(row_count, heads_here, HEAD)
    value_heads = value_rows.reshape(row_count, heads_here, HEAD)
    query_blocks = queries.reshape(blocks, QBLOCK, heads_here, HEAD)

    def block_scores(query_block, seg_block):
        scores = (
            jnp.einsum("qhd,khd->hqk", query_block, key_heads, preferred_element_type=jnp.float32)
            * score_scale
        )
        same = seg_block[:, None] == segments[None, :]
        return jnp.where(same[None], scores, -1e30)

    def forward_block(pieces):
        query_block, seg_block = pieces
        scores = block_scores(query_block, seg_block)
        row_max = jnp.max(scores, axis=-1, keepdims=True)
        raised = jnp.exp(scores - row_max)
        row_sum = jnp.sum(raised, axis=-1, keepdims=True)
        probs = raised / row_sum
        block_out = jnp.einsum(
            "hqk,khd->qhd",
            probs.astype(jnp.bfloat16),
            value_heads,
            preferred_element_type=jnp.float32,
        )
        return (block_out.astype(jnp.bfloat16), (row_max + jnp.log(row_sum))[..., 0])

    out_blocks, log_norms = lax.map(forward_block, (query_blocks, seg_blocks))
    attended = out_blocks.reshape(row_count, local_cols)
    attention_sum = lax.psum(
        jnp.dot(attended, w_out, preferred_element_type=jnp.float32).astype(jnp.bfloat16), "mp"
    ).astype(jnp.float32)
    middle = inputs + attention_sum + b_out
    norm_two, norm_two_back = jax.vjp(normalize, middle, ln2_gain, ln2_bias)
    normed_two = norm_two.astype(jnp.bfloat16)
    hidden_pre = jnp.dot(normed_two, w_fc1, preferred_element_type=jnp.float32) + b_fc1
    activated_full, gelu_back = jax.vjp(exact_gelu, hidden_pre)
    activated = activated_full.astype(jnp.bfloat16)
    mlp_sum = lax.psum(
        jnp.dot(activated, w_fc2, preferred_element_type=jnp.float32).astype(jnp.bfloat16), "mp"
    ).astype(jnp.float32)
    output = (middle + mlp_sum + b_fc2).astype(jnp.bfloat16)
    upstream = cotangent.astype(jnp.float32)
    grad_b_fc2 = jnp.sum(upstream, axis=0)
    grad_w_fc2 = jnp.einsum("tf,td->fd", activated, cotangent, preferred_element_type=jnp.float32)
    d_act = jnp.einsum("td,fd->tf", cotangent, w_fc2, preferred_element_type=jnp.float32)
    d_pre = gelu_back(d_act)[0]
    grad_b_fc1 = jnp.sum(d_pre, axis=0)
    d_pre_low = d_pre.astype(jnp.bfloat16)
    grad_w_fc1 = jnp.einsum("td,tf->df", normed_two, d_pre_low, preferred_element_type=jnp.float32)
    d_normed_two = lax.psum(
        jnp.einsum("tf,df->td", d_pre_low, w_fc1, preferred_element_type=jnp.float32).astype(
            jnp.bfloat16
        ),
        "mp",
    ).astype(jnp.float32)
    d_middle_norm, grad_ln2_gain, grad_ln2_bias = norm_two_back(d_normed_two)
    d_middle = upstream + d_middle_norm
    grad_b_out = jnp.sum(d_middle, axis=0)
    d_middle_low = d_middle.astype(jnp.bfloat16)
    grad_w_out = jnp.einsum("tc,td->cd", attended, d_middle_low, preferred_element_type=jnp.float32)
    d_attended = jnp.einsum(
        "td,cd->tc", d_middle_low, w_out, preferred_element_type=jnp.float32
    ).astype(jnp.bfloat16)
    d_att_blocks = d_attended.reshape(blocks, QBLOCK, heads_here, HEAD)

    def backward_block(running, pieces):
        d_keys_acc, d_values_acc = running
        query_block, seg_block, d_out_block, log_norm = pieces
        scores = block_scores(query_block, seg_block)
        probs = jnp.exp(scores - log_norm[..., None])
        d_probs = jnp.einsum(
            "qhd,khd->hqk", d_out_block, value_heads, preferred_element_type=jnp.float32
        )
        d_scores = probs * (d_probs - jnp.sum(probs * d_probs, axis=-1, keepdims=True))
        d_scores_low = d_scores.astype(jnp.bfloat16)
        d_query_block = (
            jnp.einsum("hqk,khd->qhd", d_scores_low, key_heads, preferred_element_type=jnp.float32)
            * score_scale
        )
        d_keys_acc = (
            d_keys_acc
            + jnp.einsum(
                "hqk,qhd->khd", d_scores_low, query_block, preferred_element_type=jnp.float32
            )
            * score_scale
        )
        d_values_acc = d_values_acc + jnp.einsum(
            "hqk,qhd->khd",
            probs.astype(jnp.bfloat16),
            d_out_block,
            preferred_element_type=jnp.float32,
        )
        return ((d_keys_acc, d_values_acc), d_query_block)

    zeros_acc = jnp.zeros((row_count, heads_here, HEAD), jnp.float32)
    (d_keys, d_values), d_query_blocks = lax.scan(
        backward_block, (zeros_acc, zeros_acc), (query_blocks, seg_blocks, d_att_blocks, log_norms)
    )
    d_queries = d_query_blocks.reshape(row_count, local_cols)
    d_keys = d_keys.reshape(row_count, local_cols)
    d_values = d_values.reshape(row_count, local_cols)
    grad_b_qv = jnp.stack([jnp.sum(d_queries, axis=0), jnp.sum(d_values, axis=0)])
    stacked = jnp.stack([d_queries, d_keys, d_values]).astype(jnp.bfloat16)
    grad_w_qkv = jnp.einsum("td,stc->sdc", normed_one, stacked, preferred_element_type=jnp.float32)
    d_normed_one = lax.psum(
        jnp.einsum("stc,sdc->td", stacked, w_qkv, preferred_element_type=jnp.float32).astype(
            jnp.bfloat16
        ),
        "mp",
    ).astype(jnp.float32)
    d_input_norm, grad_ln1_gain, grad_ln1_bias = norm_one_back(d_normed_one)
    grad_tokens = d_middle + d_input_norm
    summed_qkv, summed_out, summed_fc1, summed_fc2 = (
        lax.psum_scatter(grad_w_qkv, "dp", scatter_dimension=1, tiled=True),
        lax.psum_scatter(grad_w_out, "dp", scatter_dimension=1, tiled=True),
        lax.psum_scatter(grad_w_fc1, "dp", scatter_dimension=0, tiled=True),
        lax.psum_scatter(grad_w_fc2, "dp", scatter_dimension=1, tiled=True),
    )
    small_sums = lax.psum(
        (
            grad_ln1_gain,
            grad_ln1_bias,
            grad_ln2_gain,
            grad_ln2_bias,
            grad_b_out,
            grad_b_fc2,
            grad_b_qv,
            grad_b_fc1,
        ),
        "dp",
    )
    return (
        output,
        grad_tokens,
        summed_qkv,
        small_sums[6],
        summed_out,
        small_sums[4],
        summed_fc1,
        small_sums[7],
        summed_fc2,
        small_sums[5],
        small_sums[0],
        small_sums[1],
        small_sums[2],
        small_sums[3],
    )


def solution(mesh):
    in_specs = (
        P("dp", None),
        P("dp", None),
        P("dp", None),
        P(None, None, "mp"),
        P(None, "mp"),
        P("mp", None),
        P(),
        P(None, "mp"),
        P("mp"),
        P("mp", None),
        P(),
        P(),
        P(),
        P(),
        P(),
    )
    out_specs = (
        P("dp", None),
        P("dp", None),
        P(None, "dp", "mp"),
        P(None, "mp"),
        P("mp", "dp"),
        P(),
        P("dp", "mp"),
        P("mp"),
        P("mp", "dp"),
        P(),
        P(),
        P(),
        P(),
        P(),
    )
    return jax.shard_map(
        per_device, mesh=mesh, in_specs=in_specs, out_specs=out_specs, check_vma=False
    )
```

profile of v0, /device:TPU:0, one launch (start us, length us, event | category | flops | bytes accessed | tf_op | source)
XLA Modules:
  0.0 1066.7 jit_solution(14940275114370547031)
XLA Ops:
  23.9 4.4 reshape.241
  28.3 4.1 copy.50
  32.3 64.4 %while.27 = (s32[]{:T(128)}, bf16[4,512,4,64]{1,3,2,0:T(8,128)(2,1)}, f32[4,4,512]{2,1,0:T(4,128)}, s32[4,512]{1,0:T(4,128)S(1)}, s32[2048]{0:T(1024)S(1)}, /*in...) while((s32[]{:T(128)}, ...), condition=%wide.region_7.8_spmd, body=%wide.region_4.7_spmd.sunk | while | flops 1125251072 | bytes 61421712 | solution.py:90
  33.0 4.4 fusion.146
  37.4 4.3 fusion.147
  41.8 5.9 fusion.148
  49.0 4.4 fusion.146
  53.5 4.3 fusion.147
  57.8 5.9 fusion.148
  65.0 4.4 fusion.146
  69.5 4.3 fusion.147
  73.8 5.9 fusion.148
  81.0 4.4 fusion.146
  85.5 4.3 fusion.147
  89.8 5.9 fusion.148
  101.0 4.4 convolution_convert_fusion
  105.5 88.3 %all-reduce.6.cloned.1.call-done = bf16[2048,1024]{1,0:T(8,128)(2,1)} async-done(((bf16[2048,1024]{1,0:T(8,128)(2,1)}), bf16[2048,1024]{1,0:T(8,128)(2,1)}) %all-reduce.6.cloned.1.call-update) | async-done | bytes 4194320 | tf_op jit(solution)/shard_map/psum | solution.py:92
  193.8 5.0 fusion.65
  201.9 5.8 fusion.91
  207.7 25.4 %fusion.94 = (f32[1024]{0:T(1024)}, bf16[2048,1024]{1,0:T(8,128)(2,1)S(1)}, f32[2048,1024]{1,0:T(8,128)}) fusion(f32[2048,1024]{1,0:T(8,128)S(1)} %fusion.91, f32[1024]{0:T(1024)S(1)} %copy-done.52, bf16[2048,1024]{1,0:T(8,128)(2,1)S(1)} %copy-done.21, bf16[1024,1024]{1,0:T(8,128)(2,1)S(1)} %copy-done), kind=kOutput, calls=%fused_computation.147 | convolution fusion | flops 4450155520 | bytes 27271168 | tf_op jit(solution)/shard_map/td,fd->tf/dot_general | solution.py:108
  235.1 6.3 convolution_convert_fusion.1
  241.7 10.4 multiply_convert_fusion.1
  252.1 8.4 convolution_convert_fusion.2
  260.5 66.8 %all-reduce.8.cloned.1.call-done = bf16[2048,1024]{1,0:T(8,128)(2,1)} async-done(((bf16[2048,1024]{1,0:T(8,128)(2,1)}), bf16[2048,1024]{1,0:T(8,128)(2,1)}) %all-reduce.8.cloned.1.call-update) | async-done | bytes 4194320 | tf_op jit(solution)/shard_map/psum | solution.py:113
  327.3 8.5 convert_reduce_fusion.1
  335.8 7.0 fusion.57
  342.8 6.3 fusion.96
  360.5 195.5 %while.28 = (s32[]{:T(128)}, f32[2048,4,64]{0,2,1:T(8,128)}, f32[2048,4,64]{0,2,1:T(8,128)}, f32[4,512,4,64]{1,3,2,0:T(8,128)}, bf16[4,512,4,64]{1,3,2,0:T(8,128...) while((s32[]{:T(128)}, f32[2048,4,64]{0,2,1:T(8,128)}, ...), condition=%wide.region_17.18_spmd.clone, body=%wide.region_15.17_spmd.clone.sunk | while | flops 2751068160 | bytes 164206880 | solution.py:159
  366.5 7.2 fusion.160
  373.7 11.5 %multiply_reduce_fusion.3 = (f32[4,512]{1,0:T(4,128)}, f32[4,512,2048]{2,1,0:T(8,128)}) fusion(f32[4,512,2048]{2,1,0:T(8,128)S(1)} %fusion.158, f32[4,512]{1,0:T(4,128)S(1)} %dynamic-slice_bitcast_fusion.2, pred[512,2048]{1,0:T(8,128)(4,1)} %copy-done.8, bf16[2048,4,64]{0,2,1:T(8,128)(2,1)} %get-tuple-element.520, ...), kind=kOutput, calls=%fused_computation.19.clone.1 | convolution fusion | flops 557840384 | bytes 35930116 | tf_op jit(solution)/shard_map/while/body/eval_jaxpr/qhd,khd->hqk/dot_general | solution.py:134
  385.2 11.1 %multiply_convert_fusion.3 = bf16[4,512,2048]{2,1,0:T(8,128)(2,1)} fusion(f32[4,512,2048]{2,1,0:T(8,128)} %get-tuple-element.455, f32[4,512,2048]{2,1,0:T(8,128)S(1)} %fusion.158, f32[4,512]{1,0:T(4,128)} %get-tuple-element.456, f32[4,512]{1,0:T(4,128)S(1)} %dynamic-slice_bitcast_fusion.2, pred[512,2048]{1,0:T(8,128)(4,1)} %copy-done.8), kind=kLoop, calls=%fused_computation.18.clone.1 | loop fusion | flops 25165824 | bytes 43008000 | tf_op jit(solution)/shard_map/while/body/eval_jaxpr/convert_element_type | solution.py:138
  396.3 5.3 fusion.159
  401.6 7.7 fusion.161
  411.4 3.5 fusion.158
  414.9 7.6 fusion.160
  422.5 11.5 %multiply_reduce_fusion.3 = (f32[4,512]{1,0:T(4,128)}, f32[4,512,2048]{2,1,0:T(8,128)}) fusion(f32[4,512,2048]{2,1,0:T(8,128)S(1)} %fusion.158, f32[4,512]{1,0:T(4,128)S(1)} %dynamic-slice_bitcast_fusion.2, pred[512,2048]{1,0:T(8,128)(4,1)} %copy-done.8, bf16[2048,4,64]{0,2,1:T(8,128)(2,1)} %get-tuple-element.520, ...), kind=kOutput, calls=%fused_computation.19.clone.1 | convolution fusion | flops 557840384 | bytes 35930116 | tf_op jit(solution)/shard_map/while/body/eval_jaxpr/qhd,khd->hqk/dot_general | solution.py:134
  434.0 11.1 %multiply_convert_fusion.3 = bf16[4,512,2048]{2,1,0:T(8,128)(2,1)} fusion(f32[4,512,2048]{2,1,0:T(8,128)} %get-tuple-element.455, f32[4,512,2048]{2,1,0:T(8,128)S(1)} %fusion.158, f32[4,512]{1,0:T(4,128)} %get-tuple-element.456, f32[4,512]{1,0:T(4,128)S(1)} %dynamic-slice_bitcast_fusion.2, pred[512,2048]{1,0:T(8,128)(4,1)} %copy-done.8), kind=kLoop, calls=%fused_computation.18.clone.1 | loop fusion | flops 25165824 | bytes 43008000 | tf_op jit(solution)/shard_map/while/body/eval_jaxpr/convert_element_type | solution.py:138
  445.1 5.3 fusion.159
  450.5 7.7 fusion.161
  460.2 3.5 fusion.158
  463.7 7.6 fusion.160
  471.4 11.5 %multiply_reduce_fusion.3 = (f32[4,512]{1,0:T(4,128)}, f32[4,512,2048]{2,1,0:T(8,128)}) fusion(f32[4,512,2048]{2,1,0:T(8,128)S(1)} %fusion.158, f32[4,512]{1,0:T(4,128)S(1)} %dynamic-slice_bitcast_fusion.2, pred[512,2048]{1,0:T(8,128)(4,1)} %copy-done.8, bf16[2048,4,64]{0,2,1:T(8,128)(2,1)} %get-tuple-element.520, ...), kind=kOutput, calls=%fused_computation.19.clone.1 | convolution fusion | flops 557840384 | bytes 35930116 | tf_op jit(solution)/shard_map/while/body/eval_jaxpr/qhd,khd->hqk/dot_general | solution.py:134
  482.9 11.1 %multiply_convert_fusion.3 = bf16[4,512,2048]{2,1,0:T(8,128)(2,1)} fusion(f32[4,512,2048]{2,1,0:T(8,128)} %get-tuple-element.455, f32[4,512,2048]{2,1,0:T(8,128)S(1)} %fusion.158, f32[4,512]{1,0:T(4,128)} %get-tuple-element.456, f32[4,512]{1,0:T(4,128)S(1)} %dynamic-slice_bitcast_fusion.2, pred[512,2048]{1,0:T(8,128)(4,1)} %copy-done.8), kind=kLoop, calls=%fused_computation.18.clone.1 | loop fusion | flops 25165824 | bytes 43008000 | tf_op jit(solution)/shard_map/while/body/eval_jaxpr/convert_element_type | solution.py:138
  494.0 5.3 fusion.159
  499.3 7.7 fusion.161
  512.6 7.6 fusion.160
  520.2 11.5 %multiply_reduce_fusion.3 = (f32[4,512]{1,0:T(4,128)}, f32[4,512,2048]{2,1,0:T(8,128)}) fusion(f32[4,512,2048]{2,1,0:T(8,128)S(1)} %fusion.158, f32[4,512]{1,0:T(4,128)S(1)} %dynamic-slice_bitcast_fusion.2, pred[512,2048]{1,0:T(8,128)(4,1)} %copy-done.8, bf16[2048,4,64]{0,2,1:T(8,128)(2,1)} %get-tuple-element.520, ...), kind=kOutput, calls=%fused_computation.19.clone.1 | convolution fusion | flops 557840384 | bytes 35930116 | tf_op jit(solution)/shard_map/while/body/eval_jaxpr/qhd,khd->hqk/dot_general | solution.py:134
  531.7 11.1 %multiply_convert_fusion.3 = bf16[4,512,2048]{2,1,0:T(8,128)(2,1)} fusion(f32[4,512,2048]{2,1,0:T(8,128)} %get-tuple-element.455, f32[4,512,2048]{2,1,0:T(8,128)S(1)} %fusion.158, f32[4,512]{1,0:T(4,128)} %get-tuple-element.456, f32[4,512]{1,0:T(4,128)S(1)} %dynamic-slice_bitcast_fusion.2, pred[512,2048]{1,0:T(8,128)(4,1)} %copy-done.8), kind=kLoop, calls=%fused_computation.18.clone.1 | loop fusion | flops 25165824 | bytes 43008000 | tf_op jit(solution)/shard_map/while/body/eval_jaxpr/convert_element_type | solution.py:138
  542.8 5.3 fusion.159
  548.1 7.6 fusion.161
  568.1 7.5 bitcast_convert_fusion
  576.8 7.7 fusion.77
  584.6 5.6 fusion.71
  590.3 10.0 fusion.100
  600.7 12.4 %fusion.74 = f32[1024,1024]{1,0:T(8,128)} fusion(bf16[2048,1024]{1,0:T(8,128)(2,1)} %copy-done.57, f32[1024]{0:T(1024)S(1)} %copy-done.56, f32[1024]{0:T(1024)S(1)} %copy-done.44, f32[2048]{0:T(1024)S(1)} %copy-done.38, bf16[2048,1024]{1,0:T(8,128)(2,1)} %all-reduce.6.cloned.1.call-done, bf16[2048,1024]{1,0:T(8,128)(2,1)} %param.19, ...), kind=kOutput, calls=%fused_computation.120 | convolution fusion | flops 4313841664 | bytes 16805888 | tf_op jit(solution)/shard_map/td,tf->df/dot_general | solution.py:112
  613.3 115.5 %all-reduce.10.cloned.1.call-done = (bf16[2048,1024]{1,0:T(8,128)(2,1)}, bf16[2048,1024]{1,0:T(8,128)(2,1)}) async-done(((bf16[2048,1024]{1,0:T(8,128)(2,1)}, bf16[2048,1024]{1,0:T(8,128)(2,1)}), (bf16[2048,1024]{1,0:T(8,128)(2,1)}, bf16[2048,1024]{1,0:T(8,128)(2,1)})) %all-reduce.10.cloned.1.call-update) | async-done | bytes 8388624 | tf_op jit(solution)/shard_map/psum | solution.py:101
  728.9 5.7 convert_reduce_fusion
  734.7 5.4 fusion.58
  740.2 38.7 %all-reduce = (f32[2,256]{1,0:T(2,128)}, f32[1024]{0:T(1024)}, f32[1024]{0:T(1024)}, f32[1024]{0:T(1024)}, f32[1024]{0:T(1024)}, /*index=5*/f32[1024]{0:T(1024)}, f32[1024]{0:T(1024)}, f32[1024]{0:T(1024)}) all-reduce(f32[2,256]{1,0:T(2,128)S(1)} %pad_maximum_fusion.3, ...), channel_id=1, replica_groups=mesh['dp'=8,'mp'=4] {'dp'}, use_global_device_ids=true, to_apply=%region_24.25 | all-reduce | flops 7680 | bytes 61440 | tf_op jit(solution)/shard_map/psum | solution.py:182
  778.9 16.0 %add_add_fusion.2 = (f32[2048,1024]{1,0:T(8,128)}, bf16[2048,1024]{1,0:T(8,128)(2,1)}) fusion(f32[2048,1024]{1,0:T(8,128)} %copy-done.9, bf16[2048,1024]{1,0:T(8,128)(2,1)} %param.19, bf16[2048,1024]{1,0:T(8,128)(2,1)} %get-tuple-element.311, f32[2048]{0:T(1024)S(1)} %negate_multiply_fusion.1, f32[2048]{0:T(1024)S(1)} %multiply_multiply_fusion.5, ...), kind=kLoop, calls=%fused_computation.83 | loop fusion | flops 35651584 | bytes 37793792 | tf_op jit(solution)/shard_map/add | solution.py:175
  794.9 13.0 %reduce-scatter.5.cloned.1.call-done = f32[3,128,256]{1,2,0:T(8,128)} async-done(((f32[3,1024,256]{1,2,0:T(8,128)}), f32[3,128,256]{1,2,0:T(8,128)}) %reduce-scatter.5.cloned.1.call-update) | async-done | bytes 393232 | tf_op jit(solution)/shard_map/reduce_scatter | solution.py:177
  809.8 65.8 %reduce-scatter.7.cloned.1.call-done = f32[256,128]{1,0:T(8,128)} async-done(((f32[256,1024]{1,0:T(8,128)}), f32[256,128]{1,0:T(8,128)}) %reduce-scatter.7.cloned.1.call-update) | async-done | bytes 131088 | tf_op jit(solution)/shard_map/reduce_scatter | solution.py:178
  875.6 91.7 %reduce-scatter.11.cloned.1.call-done = f32[1024,128]{1,0:T(8,128)} async-done(((f32[1024,1024]{1,0:T(8,128)}), f32[1024,128]{1,0:T(8,128)}) %reduce-scatter.11.cloned.1.call-update) | async-done | bytes 524304 | tf_op jit(solution)/shard_map/reduce_scatter | solution.py:180
  967.3 92.2 %reduce-scatter.9.cloned.1.call-done = f32[128,1024]{1,0:T(8,128)} async-done(((f32[1024,1024]{1,0:T(8,128)}), f32[128,1024]{1,0:T(8,128)}) %reduce-scatter.9.cloned.1.call-update) | async-done | bytes 524304 | tf_op jit(solution)/shard_map/reduce_scatter | solution.py:179
  (226 shorter events, 73.9 us)
Async XLA Ops:
  7.2 200.5 %copy-start = (bf16[1024,1024]{1,0:T(8,128)(2,1)S(1)}, bf16[1024,1024]{1,0:T(8,128)(2,1)}, u32[]{:S(2)}) copy-start(bf16[1024,1024]{1,0:T(8,128)(2,1)} %param.28) | copy-start | bytes 6291460
  7.2 9.1 copy-start.41
  7.2 9.1 copy-start.49
  7.2 186.6 %all-reduce.6.cloned.1.call-start = ((), (), s32[]{:S(2)}) async-start(), calls=%async_computation.4 | async-start | bytes 8388608 | tf_op jit(solution)/shard_map/psum | solution.py:92
  9.1 7.2 copy-start.2
  9.1 8.9 copy-start.54
  37.4 4.3 copy-start.16
  97.3 8.1 copy-start.6
  97.3 8.1 copy-start.24
  97.3 96.4 %copy-start.32 = (f32[1024]{0:T(1024)S(1)}, f32[1024]{0:T(1024)}, u32[]{:S(2)}) copy-start(f32[1024]{0:T(1024)} %param.25) | copy-start | bytes 12292
  105.4 96.4 %copy-start.43 = (f32[1024]{0:T(1024)S(1)}, f32[1024]{0:T(1024)}, u32[]{:S(2)}) copy-start(f32[1024]{0:T(1024)} %param.32) | copy-start | bytes 12292
  105.4 96.4 %copy-start.55 = (f32[1024]{0:T(1024)S(1)}, f32[1024]{0:T(1024)}, u32[]{:S(2)}) copy-start(f32[1024]{0:T(1024)} %param.33) | copy-start | bytes 12292
  105.5 221.8 %all-reduce.8.cloned.1.call-start = ((), (), s32[]{:S(2)}) async-start(), calls=%async_computation.5 | async-start | bytes 8388608 | tf_op jit(solution)/shard_map/psum | solution.py:113
  193.8 5.1 copy-start.3
  193.8 5.9 copy-start.10
  193.8 8.1 copy-start.53
  199.7 143.1 %copy-start.30 = (f32[2048]{0:T(1024)}, f32[2048]{0:T(1024)S(1)}, u32[]{:S(2)}) copy-start(f32[2048]{0:T(1024)S(1)} %broadcast_multiply_fusion) | copy-start | bytes 24580
  201.8 140.9 %copy-start.37 = (f32[2048]{0:T(1024)}, f32[2048]{0:T(1024)S(1)}, u32[]{:S(2)}) copy-start(f32[2048]{0:T(1024)S(1)} %fusion.87) | copy-start | bytes 24580
  201.9 5.8 copy-start.21
  201.9 5.8 copy-start.52
  207.7 25.4 %copy-start.19 = (f32[2048,1024]{1,0:T(8,128)}, f32[2048,1024]{1,0:T(8,128)S(1)}, u32[]{:S(2)}) copy-start(f32[2048,1024]{1,0:T(8,128)S(1)} %fusion.91) | copy-start | bytes 25165828
  241.5 487.3 %all-reduce.10.cloned.1.call-start = ((), (), s32[]{:S(2)}) async-start(), calls=%async_computation.10 | async-start | bytes 16777216 | tf_op jit(solution)/shard_map/psum | solution.py:101
  327.2 8.5 copy-start.4
  327.2 8.5 copy-start.11
  327.3 8.5 copy-start.15
  335.8 7.0 copy-start.22
  342.8 9.8 copy-start.23
  352.5 7.9 copy-start.7
  352.5 7.9 copy-start.25
  385.2 11.1 %copy-start.12 = (f32[2048,4,64]{0,2,1:T(8,128)S(1)}, f32[2048,4,64]{0,2,1:T(8,128)}, u32[]{:S(2)}) copy-start(f32[2048,4,64]{0,2,1:T(8,128)} %get-tuple-element.498) | copy-start | bytes 6291460 | tf_op jit(solution)/shard_map/while
  396.3 13.0 %copy-start.26 = (s32[2048]{0:T(1024)S(1)}, s32[2048]{0:T(1024)}, u32[]{:S(2)}) copy-start(s32[2048]{0:T(1024)} %get-tuple-element.570) | copy-start | bytes 24580 | tf_op jit(solution)/shard_map/while
  401.6 7.7 copy-start.13
  434.0 11.1 %copy-start.12 = (f32[2048,4,64]{0,2,1:T(8,128)S(1)}, f32[2048,4,64]{0,2,1:T(8,128)}, u32[]{:S(2)}) copy-start(f32[2048,4,64]{0,2,1:T(8,128)} %get-tuple-element.498) | copy-start | bytes 6291460 | tf_op jit(solution)/shard_map/while
  445.1 13.0 %copy-start.26 = (s32[2048]{0:T(1024)S(1)}, s32[2048]{0:T(1024)}, u32[]{:S(2)}) copy-start(s32[2048]{0:T(1024)} %get-tuple-element.570) | copy-start | bytes 24580 | tf_op jit(solution)/shard_map/while
  450.4 7.7 copy-start.13
  482.8 11.1 %copy-start.12 = (f32[2048,4,64]{0,2,1:T(8,128)S(1)}, f32[2048,4,64]{0,2,1:T(8,128)}, u32[]{:S(2)}) copy-start(f32[2048,4,64]{0,2,1:T(8,128)} %get-tuple-element.498) | copy-start | bytes 6291460 | tf_op jit(solution)/shard_map/while
  494.0 13.0 %copy-start.26 = (s32[2048]{0:T(1024)S(1)}, s32[2048]{0:T(1024)}, u32[]{:S(2)}) copy-start(s32[2048]{0:T(1024)} %get-tuple-element.570) | copy-start | bytes 24580 | tf_op jit(solution)/shard_map/while
  499.3 7.7 copy-start.13
  531.7 11.1 %copy-start.12 = (f32[2048,4,64]{0,2,1:T(8,128)S(1)}, f32[2048,4,64]{0,2,1:T(8,128)}, u32[]{:S(2)}) copy-start(f32[2048,4,64]{0,2,1:T(8,128)} %get-tuple-element.498) | copy-start | bytes 6291460 | tf_op jit(solution)/shard_map/while
  542.8 13.0 %copy-start.26 = (s32[2048]{0:T(1024)S(1)}, s32[2048]{0:T(1024)}, u32[]{:S(2)}) copy-start(s32[2048]{0:T(1024)} %get-tuple-element.570) | copy-start | bytes 24580 | tf_op jit(solution)/shard_map/while
  548.1 7.7 copy-start.13
  575.6 8.9 copy-start.18
  575.6 232.3 %reduce-scatter.5.cloned.1.call-start = ((), (), s32[]{:S(2)}) async-start(), calls=%async_computation.6 | async-start | bytes 3538944 | tf_op jit(solution)/shard_map/reduce_scatter | solution.py:177
  584.5 291.1 %reduce-scatter.7.cloned.1.call-start = ((), (), s32[]{:S(2)}) async-start(), calls=%async_computation.7 | async-start | bytes 1179648 | tf_op jit(solution)/shard_map/reduce_scatter | solution.py:178
  590.2 10.4 copy-start.31
  590.2 10.4 copy-start.33
  590.2 10.4 copy-start.38
  590.2 10.4 copy-start.44
  590.2 10.4 copy-start.56
  590.3 377.0 %reduce-scatter.11.cloned.1.call-start = ((), (), s32[]{:S(2)}) async-start(), calls=%async_computation.9 | async-start | bytes 4718592 | tf_op jit(solution)/shard_map/reduce_scatter | solution.py:180
  600.3 128.5 %copy-start.29 = (f32[2048]{0:T(1024)S(1)}, f32[2048]{0:T(1024)}, u32[]{:S(2)}) copy-start(f32[2048]{0:T(1024)} %copy-done.28) | copy-start | bytes 24580
  600.4 128.5 %copy-start.42 = (f32[1024]{0:T(1024)S(1)}, f32[1024]{0:T(1024)}, u32[]{:S(2)}) copy-start(f32[1024]{0:T(1024)} %param.30) | copy-start | bytes 12292
  600.4 459.1 %reduce-scatter.9.cloned.1.call-start = ((), (), s32[]{:S(2)}) async-start(), calls=%async_computation.8 | async-start | bytes 4718592 | tf_op jit(solution)/shard_map/reduce_scatter | solution.py:179
  613.1 121.4 %copy-start.40 = (f32[2048]{0:T(1024)S(1)}, f32[2048]{0:T(1024)}, u32[]{:S(2)}) copy-start(f32[2048]{0:T(1024)} %copy-done.39) | copy-start | bytes 24580
  613.1 121.5 %copy-start.35 = (f32[2048]{0:T(1024)S(1)}, f32[2048]{0:T(1024)}, u32[]{:S(2)}) copy-start(f32[2048]{0:T(1024)} %copy-done.34) | copy-start | bytes 24580
  728.8 5.8 copy-start.5
  728.8 5.9 copy-start.14
  728.8 11.3 %copy-start.45 = (f32[1024]{0:T(1024)S(1)}, f32[1024]{0:T(1024)}, u32[]{:S(2)}) copy-start(f32[1024]{0:T(1024)} %get-tuple-element.260) | copy-start | bytes 12292
  728.8 11.3 %copy-start.46 = (f32[1024]{0:T(1024)S(1)}, f32[1024]{0:T(1024)}, u32[]{:S(2)}) copy-start(f32[1024]{0:T(1024)} %get-tuple-element.256) | copy-start | bytes 12292
  728.8 11.3 %copy-start.47 = (f32[1024]{0:T(1024)S(1)}, f32[1024]{0:T(1024)}, u32[]{:S(2)}) copy-start(f32[1024]{0:T(1024)} %get-tuple-element.315) | copy-start | bytes 12292
  728.8 11.3 %copy-start.48 = (f32[1024]{0:T(1024)S(1)}, f32[1024]{0:T(1024)}, u32[]{:S(2)}) copy-start(f32[1024]{0:T(1024)} %get-tuple-element.321) | copy-start | bytes 12292
  728.9 11.3 %copy-start.51 = (f32[1024]{0:T(1024)S(1)}, f32[1024]{0:T(1024)}, u32[]{:S(2)}) copy-start(f32[1024]{0:T(1024)} %get-tuple-element.312) | copy-start | bytes 12292
  728.9 50.0 %copy-start.50 = (f32[1024]{0:T(1024)S(1)}, f32[1024]{0:T(1024)}, u32[]{:S(2)}) copy-start(f32[1024]{0:T(1024)} %param.29) | copy-start | bytes 12292
  778.9 280.6 %copy-start.1 = (bf16[1024,1024]{1,0:T(8,128)(2,1)S(1)}, bf16[1024,1024]{1,0:T(8,128)(2,1)}, u32[]{:S(2)}) copy-start(bf16[1024,1024]{1,0:T(8,128)(2,1)} %param.28) | copy-start | bytes 6291460
  (16 other events, 43.3 us)
Sparse Core Ops, SparseCore 0:
  105.5 88.1 all-reduce.5
  241.6 85.6 all-reduce.7
  575.7 153.0 all-reduce.9
  732.3 75.5 reduce-scatter.4
  811.7 63.8 reduce-scatter.6
  879.6 87.6 reduce-scatter.10
  971.5 87.9 reduce-scatter.8
where the time goes:
time: 1080 us; the launch traced here: 1070 us
  waiting for transfers between devices  533 us (49%)
  matrix products  285 us (26%)
  other arithmetic  151 us (14%)
  local copies, waits for them, and re-layouts  41.2 us (4%)
  blocking collectives  38.7 us (4%)
  between operations  15.2 us (1%)
    psum x1, waiting for transfers between devices, per_device(): lax.psum(jnp.dot(activated, w_fc2, preferred_element_type=jnp.float32).as...  115 us
    reduce_scatter x1, waiting for transfers between devices, per_device(): lax.psum_scatter(grad_w_fc1, 'dp', scatter_dimension=0, tiled=True)  92.2 us
    reduce_scatter x1, waiting for transfers between devices, per_device(): lax.psum_scatter(grad_w_fc2, 'dp', scatter_dimension=1, tiled=True)  91.7 us
    psum x1, waiting for transfers between devices, per_device(): lax.psum(jnp.dot(attended, w_out, preferred_element_type=jnp.float32).ast...  88.3 us
    psum x1, waiting for transfers between devices, per_device(): lax.psum(jnp.einsum('tf,df->td', d_pre_low, w_fc1, preferred_element_type...  66.8 us
    reduce_scatter x1, waiting for transfers between devices, per_device(): lax.psum_scatter(grad_w_out, 'dp', scatter_dimension=1, tiled=True)  65.8 us
    dot_general x4, matrix products, backward_block(): jnp.einsum('qhd,khd->hqk', d_out_block, value_heads, preferred_element_ty...  45.9 us
    convert_element_type x4, other arithmetic, backward_block(): d_scores_low = d_scores.astype(jnp.bfloat16)  44.5 us
  transfers between devices with their start and end apart: 7, of which 7 were waited for; matrix products, arithmetic and copies ran while one was open for 8% of the time, Pallas kernels for 0%

commit v1 on v0

--- a/solution.py
+++ b/solution.py
@@ -1,3 +1,5 @@
+from functools import partial
+
 import jax
 import jax.numpy as jnp
 from jax import lax
@@ -24,7 +26,26 @@
     return jnp.sum((positions[:, None] >= ends[None, :]).astype(jnp.int32), axis=1)
 
 
-def per_device(
+def mp_allreduce(partial, n_mp):
+    if n_mp != 4:
+        return lax.psum(partial, "mp").astype(jnp.float32)
+    idx = lax.axis_index("mp")
+    low_bit = idx % 2
+    half = partial.shape[0] // 2
+    mine = lax.dynamic_slice_in_dim(partial, low_bit * half, half, 0)
+    other = lax.dynamic_slice_in_dim(partial, (1 - low_bit) * half, half, 0)
+    got = lax.ppermute(other, "mp", [(k, k ^ 1) for k in range(4)])
+    first = (mine.astype(jnp.float32) + got.astype(jnp.float32)).astype(jnp.bfloat16)
+    got_far = lax.ppermute(first, "mp", [(k, k ^ 2) for k in range(4)])
+    second = (first.astype(jnp.float32) + got_far.astype(jnp.float32)).astype(jnp.bfloat16)
+    got_back = lax.ppermute(second, "mp", [(k, k ^ 1) for k in range(4)])
+    top = jnp.where(low_bit == 0, second, got_back)
+    bottom = jnp.where(low_bit == 0, got_back, second)
+    return jnp.concatenate([top, bottom], axis=0).astype(jnp.float32)
+
+
+def per_device(n_mp,
+
     tokens,
     cotangent,
     item_lengths,
@@ -89,18 +110,18 @@
 
     out_blocks, log_norms = lax.map(forward_block, (query_blocks, seg_blocks))
     attended = out_blocks.reshape(row_count, local_cols)
-    attention_sum = lax.psum(
-        jnp.dot(attended, w_out, preferred_element_type=jnp.float32).astype(jnp.bfloat16), "mp"
-    ).astype(jnp.float32)
+    attention_sum = mp_allreduce(
+        jnp.dot(attended, w_out, preferred_element_type=jnp.float32).astype(jnp.bfloat16), n_mp
+    )
     middle = inputs + attention_sum + b_out
     norm_two, norm_two_back = jax.vjp(normalize, middle, ln2_gain, ln2_bias)
     normed_two = norm_two.astype(jnp.bfloat16)
     hidden_pre = jnp.dot(normed_two, w_fc1, preferred_element_type=jnp.float32) + b_fc1
     activated_full, gelu_back = jax.vjp(exact_gelu, hidden_pre)
     activated = activated_full.astype(jnp.bfloat16)
-    mlp_sum = lax.psum(
-        jnp.dot(activated, w_fc2, preferred_element_type=jnp.float32).astype(jnp.bfloat16), "mp"
-    ).astype(jnp.float32)
+    mlp_sum = mp_allreduce(
+        jnp.dot(activated, w_fc2, preferred_element_type=jnp.float32).astype(jnp.bfloat16), n_mp
+    )
     output = (middle + mlp_sum + b_fc2).astype(jnp.bfloat16)
     upstream = cotangent.astype(jnp.float32)
     grad_b_fc2 = jnp.sum(upstream, axis=0)
@@ -110,12 +131,12 @@
     grad_b_fc1 = jnp.sum(d_pre, axis=0)
     d_pre_low = d_pre.astype(jnp.bfloat16)
     grad_w_fc1 = jnp.einsum("td,tf->df", normed_two, d_pre_low, preferred_element_type=jnp.float32)
-    d_normed_two = lax.psum(
+    d_normed_two = mp_allreduce(
         jnp.einsum("tf,df->td", d_pre_low, w_fc1, preferred_element_type=jnp.float32).astype(
             jnp.bfloat16
         ),
-        "mp",
-    ).astype(jnp.float32)
+        n_mp,
+    )
     d_middle_norm, grad_ln2_gain, grad_ln2_bias = norm_two_back(d_normed_two)
     d_middle = upstream + d_middle_norm
     grad_b_out = jnp.sum(d_middle, axis=0)
@@ -165,48 +186,56 @@
     grad_b_qv = jnp.stack([jnp.sum(d_queries, axis=0), jnp.sum(d_values, axis=0)])
     stacked = jnp.stack([d_queries, d_keys, d_values]).astype(jnp.bfloat16)
     grad_w_qkv = jnp.einsum("td,stc->sdc", normed_one, stacked, preferred_element_type=jnp.float32)
-    d_normed_one = lax.psum(
+    d_normed_one = mp_allreduce(
         jnp.einsum("stc,sdc->td", stacked, w_qkv, preferred_element_type=jnp.float32).astype(
             jnp.bfloat16
         ),
-        "mp",
-    ).astype(jnp.float32)
+        n_mp,
+    )
     d_input_norm, grad_ln1_gain, grad_ln1_bias = norm_one_back(d_normed_one)
     grad_tokens = d_middle + d_input_norm
-    summed_qkv, summed_out, summed_fc1, summed_fc2 = (
-        lax.psum_scatter(grad_w_qkv, "dp", scatter_dimension=1, tiled=True),
-        lax.psum_scatter(grad_w_out, "dp", scatter_dimension=1, tiled=True),
-        lax.psum_scatter(grad_w_fc1, "dp", scatter_dimension=0, tiled=True),
-        lax.psum_scatter(grad_w_fc2, "dp", scatter_dimension=1, tiled=True),
-    )
-    small_sums = lax.psum(
-        (
+    def scatter(grad, dim):
+        return lax.psum_scatter(
+            grad.astype(jnp.bfloat16), "dp", scatter_dimension=dim, tiled=True
+        ).astype(jnp.float32)
+
+    summed_qkv = scatter(grad_w_qkv, 1)
+    summed_out = scatter(grad_w_out, 1)
+    summed_fc1 = scatter(grad_w_fc1, 0)
+    summed_fc2 = scatter(grad_w_fc2, 1)
+    packed = jnp.concatenate(
+        [
             grad_ln1_gain,
             grad_ln1_bias,
             grad_ln2_gain,
             grad_ln2_bias,
             grad_b_out,
             grad_b_fc2,
-            grad_b_qv,
+            grad_b_qv.reshape(-1),
             grad_b_fc1,
-        ),
-        "dp",
-    )
+        ]
+    )
+    packed = lax.psum(packed, "dp")
+    width = grad_ln1_gain.shape[0]
+    pieces = [packed[k * width : (k + 1) * width] for k in range(6)]
+    qv_size = grad_b_qv.size
+    summed_b_qv = packed[6 * width : 6 * width + qv_size].reshape(grad_b_qv.shape)
+    summed_b_fc1 = packed[6 * width + qv_size :]
     return (
         output,
         grad_tokens,
         summed_qkv,
-        small_sums[6],
+        summed_b_qv,
         summed_out,
-        small_sums[4],
+        pieces[4],
         summed_fc1,
-        small_sums[7],
+        summed_b_fc1,
         summed_fc2,
-        small_sums[5],
-        small_sums[0],
-        small_sums[1],
-        small_sums[2],
-        small_sums[3],
+        pieces[5],
+        pieces[0],
+        pieces[1],
+        pieces[2],
+        pieces[3],
     )
 
 
@@ -245,5 +274,5 @@
         P(),
     )
     return jax.shard_map(
-        per_device, mesh=mesh, in_specs=in_specs, out_specs=out_specs, check_vma=False
-    )
+        partial(per_device, mesh.shape["mp"]), mesh=mesh, in_specs=in_specs, out_specs=out_specs, check_vma=False
+    )

time: 1080 us -> 828 us (0.77)
  waiting for transfers between devices: 533 us -> 239 us
  other arithmetic: 151 us -> 182 us
  local copies, waits for them, and re-layouts: 41.2 us -> 61.1 us
    psum x3 -> x0, waiting for transfers between devices: 270 us -> none  [the longest x1 115 us: per_device(): lax.psum(jnp.dot(activated, w_fc2, preferred_element_type=jnp.float32).as...]
    reduce_scatter x4 -> x1, waiting for transfers between devices: 263 us -> 0.01 us  [scatter(): lax.psum_scatter(grad.astype(jnp.bfloat16), 'dp', scatter_dimension=dim,...]
    ppermute x0 -> x12, waiting for transfers between devices: none -> 158 us  [the longest x4 145 us: mp_allreduce(): got_far = lax.ppermute(first, 'mp', [(k, k ^ 2) for k in range(4)])]
    unnamed x7, waiting for transfers between devices: 0.11 us -> 80.9 us
    convert_element_type x0 -> x11, other arithmetic: none -> 24.3 us  [the longest x4 11.6 us: mp_allreduce(): (first.astype(jnp.float32) + got_far.astype(jnp.float32)).astype(jnp.bflo...]
    unnamed x109 -> x125, local copies, waits for them, and re-layouts: 15 us -> 30.4 us
  transfers between devices with their start and end apart: 7 -> 16, of which waited for: 7 -> 9; matrix products, arithmetic and copies ran while one was open for 8% -> 40% of each run, Pallas kernels for 0% -> 0%
where the time goes in v1:
time: 828 us; the launch traced here: 818 us
  matrix products  276 us (33%)
  waiting for transfers between devices  239 us (29%)
  other arithmetic  182 us (22%)
  local copies, waits for them, and re-layouts  61.1 us (7%)
  blocking collectives  34.7 us (4%)
  between operations  14.9 us (2%)
  starting transfers between devices  9.39 us (1%)
    ppermute x4, waiting for transfers between devices, mp_allreduce(): got_far = lax.ppermute(first, 'mp', [(k, k ^ 2) for k in range(4)])  145 us
    unnamed x7, waiting for transfers between devices  80.9 us
    dot_general x4, matrix products, backward_block(): jnp.einsum('qhd,khd->hqk', d_out_block, value_heads, preferred_element_ty...  46 us
    convert_element_type x4, other arithmetic, backward_block(): d_scores_low = d_scores.astype(jnp.bfloat16)  44.5 us
    psum x1, blocking collectives, per_device(): packed = lax.psum(packed, 'dp')  34.7 us
    dot_general x8, matrix products, block_scores(): jnp.einsum('qhd,khd->hqk', query_block, key_heads, preferred_element_type...  31.8 us
    dot_general x4, matrix products, backward_block(): jnp.einsum('hqk,khd->qhd', d_scores_low, key_heads, preferred_element_typ...  30.6 us
    unnamed x125, local copies, waits for them, and re-layouts  30.4 us
  transfers between devices with their start and end apart: 16, of which 9 were waited for; matrix products, arithmetic and copies ran while one was open for 40% of the time, Pallas kernels for 0%

profile of v1, /device:TPU:0, one launch (start us, length us, event | category | flops | bytes accessed | tf_op | source)
XLA Modules:
  0.0 818.0 jit_solution(1069003523429425183)
XLA Ops:
  24.0 4.4 reshape.260
  28.4 4.0 copy.62
  32.4 64.5 %while.27 = (s32[]{:T(128)}, bf16[4,512,4,64]{1,3,2,0:T(8,128)(2,1)}, f32[4,4,512]{2,1,0:T(4,128)}, s32[4,512]{1,0:T(4,128)S(1)}, s32[2048]{0:T(1024)S(1)}, /*in...) while((s32[]{:T(128)}, ...), condition=%wide.region_7.8_spmd, body=%wide.region_4.7_spmd.sunk | while | flops 1125251072 | bytes 61421712 | solution.py:111
  33.1 4.4 fusion.155
  37.5 4.3 fusion.156
  41.8 5.9 fusion.157
  49.1 4.4 fusion.155
  53.5 4.3 fusion.156
  57.9 5.9 fusion.157
  65.1 4.4 fusion.155
  69.5 4.3 fusion.156
  73.9 5.9 fusion.157
  81.1 4.4 fusion.155
  85.6 4.3 fusion.156
  89.9 5.9 fusion.157
  107.3 4.1 collective-permute-done
  117.6 45.9 %collective-permute-done.1 = bf16[1024,1024]{1,0:T(8,128)(2,1)S(1)} collective-permute-done((bf16[1024,1024]{1,0:T(8,128)(2,1)S(1)}, bf16[1024,1024]{1,0:T(8,128)(2,1)S(1)}, u32[]{:S(2)}, u32[]{:S(2)}) %collective-permute-start.1) | collective-permute-done | bytes 2097184 | tf_op jit(solution)/shard_map/ppermute | solution.py:39
  165.8 4.5 collective-permute-done.2
  178.7 5.8 fusion.100
  184.5 25.6 %fusion.103 = (f32[1024]{0:T(1024)}, bf16[2048,1024]{1,0:T(8,128)(2,1)}, f32[2048,1024]{1,0:T(8,128)}) fusion(f32[2048,1024]{1,0:T(8,128)S(1)} %fusion.100, f32[1024]{0:T(1024)S(1)} %copy-done.54, bf16[2048,1024]{1,0:T(8,128)(2,1)S(1)} %copy-done.22, bf16[1024,1024]{1,0:T(8,128)(2,1)S(1)} %copy-done), kind=kOutput, calls=%fused_computation.182 | convolution fusion | flops 4450155520 | bytes 27271168 | tf_op jit(solution)/shard_map/td,fd->tf/dot_general | solution.py:129
  210.1 10.1 %multiply_convert_fusion.1 = bf16[2048,1024]{1,0:T(8,128)(2,1)} fusion(f32[2048,1024]{1,0:T(8,128)} %get-tuple-element.335, f32[2048,1024]{1,0:T(8,128)} %copy-done.21, f32[1024]{0:T(1024)S(1)} %copy-done.54), kind=kLoop, calls=%fused_computation.86 | loop fusion | flops 8388608 | bytes 20975616 | tf_op jit(solution)/shard_map/convert_element_type | solution.py:121
  220.2 7.2 convolution_convert_fusion.1
  231.0 5.9 convolution_convert_fusion.5
  236.9 3.9 copy.81
  240.9 7.6 convolution_convert_fusion.2
  257.0 43.6 %collective-permute-done.7 = bf16[1024,1024]{1,0:T(8,128)(2,1)S(1)} collective-permute-done((bf16[1024,1024]{1,0:T(8,128)(2,1)S(1)}, bf16[1024,1024]{1,0:T(8,128)(2,1)S(1)}, u32[]{:S(2)}, u32[]{:S(2)}) %collective-permute-start.7) | collective-permute-done | bytes 2097184 | tf_op jit(solution)/shard_map/ppermute | solution.py:39
  302.9 11.1 %fusion.77 = bf16[1024,1024]{1,0:T(8,128)(2,1)} fusion(bf16[2048,1024]{1,0:T(8,128)(2,1)} %get-tuple-element.334, f32[1024]{0:T(1024)S(1)} %copy-done.57, f32[1024]{0:T(1024)S(1)} %copy-done.46, f32[2048]{0:T(1024)S(1)} %fusion.96, bf16[2048,1024]{1,0:T(8,128)(2,1)} %param.19, f32[2048]{0:T(1024)S(1)} %broadcast_multiply_fusion, f32[1024]{0:T(1024)S(1)} %copy-done.38, ...), kind=kOutput, calls=%fused_computation.142 | convolution fusion | flops 4321181696 | bytes 14708736 | tf_op jit(solution)/shard_map/td,tf->df/dot_general | solution.py:133
  314.2 30.5 %collective-permute-done.4 = bf16[1024,1024]{1,0:T(8,128)(2,1)} collective-permute-done((bf16[1024,1024]{1,0:T(8,128)(2,1)}, bf16[1024,1024]{1,0:T(8,128)(2,1)}, u32[]{:S(2)}, u32[]{:S(2)}) %collective-permute-start.4) | collective-permute-done | bytes 2097184 | tf_op jit(solution)/shard_map/ppermute | solution.py:39
  350.6 6.4 fusion.52
  357.1 9.5 %fusion.57 = (f32[1024]{0:T(1024)}, f32[2048]{0:T(1024)S(1)}, f32[1024]{0:T(1024)}) fusion(f32[2048]{0:T(1024)S(1)} %fusion.96, bf16[1024,1024]{1,0:T(8,128)(2,1)S(1)} %get-tuple-element.347, bf16[1024,1024]{1,0:T(8,128)(2,1)S(1)} %get-tuple-element.346, f32[2048]{0:T(1024)S(1)} %broadcast_multiply_fusion, f32[1024]{0:T(1024)S(1)} %copy-done.38, ...), kind=kLoop, calls=%fused_computation.80 | loop fusion | flops 46133248 | bytes 12632064 | tf_op jit(solution)/shard_map/transpose(jvp())/reduce_sum | solution.py:16
  366.9 11.7 %fusion.105 = (f32[1024]{0:T(1024)}, f32[2048,1024]{1,0:T(8,128)S(1)}, bf16[2048,1024]{1,0:T(8,128)(2,1)}, f32[1024]{0:T(1024)}) fusion(f32[2048]{0:T(1024)S(1)} %negate_multiply_fusion.2, f32[2048]{0:T(1024)S(1)} %multiply_multiply_fusion.6, f32[2048]{0:T(1024)S(1)} %broadcast_multiply_fusion, f32[1024]{0:T(1024)S(1)} %copy-done.38, ...), kind=kLoop, calls=%fused_computation.183 | loop fusion | flops 60815360 | bytes 33607680 | tf_op jit(solution)/shard_map/reduce_sum | solution.py:142
  390.1 195.7 %while.28 = (s32[]{:T(128)}, f32[2048,4,64]{0,2,1:T(8,128)}, f32[2048,4,64]{0,2,1:T(8,128)}, f32[4,512,4,64]{1,3,2,0:T(8,128)}, bf16[4,512,4,64]{1,3,2,0:T(8,128...) while((s32[]{:T(128)}, f32[2048,4,64]{0,2,1:T(8,128)}, ...), condition=%wide.region_14.15_spmd.clone, body=%wide.region_12.14_spmd.clone.sunk | while | flops 2751068160 | bytes 164206880 | solution.py:180
  395.9 7.3 fusion.169
  403.2 11.5 %multiply_reduce_fusion.3 = (f32[4,512]{1,0:T(4,128)}, f32[4,512,2048]{2,1,0:T(8,128)}) fusion(f32[4,512,2048]{2,1,0:T(8,128)S(1)} %fusion.167, f32[4,512]{1,0:T(4,128)S(1)} %dynamic-slice_bitcast_fusion.2, pred[512,2048]{1,0:T(8,128)(4,1)} %copy-done.8, bf16[2048,4,64]{0,2,1:T(8,128)(2,1)} %get-tuple-element.555, ...), kind=kOutput, calls=%fused_computation.19.clone.1 | convolution fusion | flops 557840384 | bytes 35930116 | tf_op jit(solution)/shard_map/while/body/eval_jaxpr/qhd,khd->hqk/dot_general | solution.py:155
  414.6 11.1 %multiply_convert_fusion.3 = bf16[4,512,2048]{2,1,0:T(8,128)(2,1)} fusion(f32[4,512,2048]{2,1,0:T(8,128)} %get-tuple-element.490, f32[4,512,2048]{2,1,0:T(8,128)S(1)} %fusion.167, f32[4,512]{1,0:T(4,128)} %get-tuple-element.491, f32[4,512]{1,0:T(4,128)S(1)} %dynamic-slice_bitcast_fusion.2, pred[512,2048]{1,0:T(8,128)(4,1)} %copy-done.8), kind=kLoop, calls=%fused_computation.18.clone.1 | loop fusion | flops 25165824 | bytes 43008000 | tf_op jit(solution)/shard_map/while/body/eval_jaxpr/convert_element_type | solution.py:159
  425.8 5.3 fusion.168
  431.1 7.6 fusion.170
  444.4 7.7 fusion.169
  452.0 11.5 %multiply_reduce_fusion.3 = (f32[4,512]{1,0:T(4,128)}, f32[4,512,2048]{2,1,0:T(8,128)}) fusion(f32[4,512,2048]{2,1,0:T(8,128)S(1)} %fusion.167, f32[4,512]{1,0:T(4,128)S(1)} %dynamic-slice_bitcast_fusion.2, pred[512,2048]{1,0:T(8,128)(4,1)} %copy-done.8, bf16[2048,4,64]{0,2,1:T(8,128)(2,1)} %get-tuple-element.555, ...), kind=kOutput, calls=%fused_computation.19.clone.1 | convolution fusion | flops 557840384 | bytes 35930116 | tf_op jit(solution)/shard_map/while/body/eval_jaxpr/qhd,khd->hqk/dot_general | solution.py:155
  463.5 11.1 %multiply_convert_fusion.3 = bf16[4,512,2048]{2,1,0:T(8,128)(2,1)} fusion(f32[4,512,2048]{2,1,0:T(8,128)} %get-tuple-element.490, f32[4,512,2048]{2,1,0:T(8,128)S(1)} %fusion.167, f32[4,512]{1,0:T(4,128)} %get-tuple-element.491, f32[4,512]{1,0:T(4,128)S(1)} %dynamic-slice_bitcast_fusion.2, pred[512,2048]{1,0:T(8,128)(4,1)} %copy-done.8), kind=kLoop, calls=%fused_computation.18.clone.1 | loop fusion | flops 25165824 | bytes 43008000 | tf_op jit(solution)/shard_map/while/body/eval_jaxpr/convert_element_type | solution.py:159
  474.7 5.3 fusion.168
  480.0 7.7 fusion.170
  493.3 7.7 fusion.169
  500.9 11.5 %multiply_reduce_fusion.3 = (f32[4,512]{1,0:T(4,128)}, f32[4,512,2048]{2,1,0:T(8,128)}) fusion(f32[4,512,2048]{2,1,0:T(8,128)S(1)} %fusion.167, f32[4,512]{1,0:T(4,128)S(1)} %dynamic-slice_bitcast_fusion.2, pred[512,2048]{1,0:T(8,128)(4,1)} %copy-done.8, bf16[2048,4,64]{0,2,1:T(8,128)(2,1)} %get-tuple-element.555, ...), kind=kOutput, calls=%fused_computation.19.clone.1 | convolution fusion | flops 557840384 | bytes 35930116 | tf_op jit(solution)/shard_map/while/body/eval_jaxpr/qhd,khd->hqk/dot_general | solution.py:155
  512.4 11.1 %multiply_convert_fusion.3 = bf16[4,512,2048]{2,1,0:T(8,128)(2,1)} fusion(f32[4,512,2048]{2,1,0:T(8,128)} %get-tuple-element.490, f32[4,512,2048]{2,1,0:T(8,128)S(1)} %fusion.167, f32[4,512]{1,0:T(4,128)} %get-tuple-element.491, f32[4,512]{1,0:T(4,128)S(1)} %dynamic-slice_bitcast_fusion.2, pred[512,2048]{1,0:T(8,128)(4,1)} %copy-done.8), kind=kLoop, calls=%fused_computation.18.clone.1 | loop fusion | flops 25165824 | bytes 43008000 | tf_op jit(solution)/shard_map/while/body/eval_jaxpr/convert_element_type | solution.py:159
  523.6 5.3 fusion.168
  528.9 7.6 fusion.170
  542.1 7.7 fusion.169
  549.8 11.5 %multiply_reduce_fusion.3 = (f32[4,512]{1,0:T(4,128)}, f32[4,512,2048]{2,1,0:T(8,128)}) fusion(f32[4,512,2048]{2,1,0:T(8,128)S(1)} %fusion.167, f32[4,512]{1,0:T(4,128)S(1)} %dynamic-slice_bitcast_fusion.2, pred[512,2048]{1,0:T(8,128)(4,1)} %copy-done.8, bf16[2048,4,64]{0,2,1:T(8,128)(2,1)} %get-tuple-element.555, ...), kind=kOutput, calls=%fused_computation.19.clone.1 | convolution fusion | flops 557840384 | bytes 35930116 | tf_op jit(solution)/shard_map/while/body/eval_jaxpr/qhd,khd->hqk/dot_general | solution.py:155
  561.3 11.1 %multiply_convert_fusion.3 = bf16[4,512,2048]{2,1,0:T(8,128)(2,1)} fusion(f32[4,512,2048]{2,1,0:T(8,128)} %get-tuple-element.490, f32[4,512,2048]{2,1,0:T(8,128)S(1)} %fusion.167, f32[4,512]{1,0:T(4,128)} %get-tuple-element.491, f32[4,512]{1,0:T(4,128)S(1)} %dynamic-slice_bitcast_fusion.2, pred[512,2048]{1,0:T(8,128)(4,1)} %copy-done.8), kind=kLoop, calls=%fused_computation.18.clone.1 | loop fusion | flops 25165824 | bytes 43008000 | tf_op jit(solution)/shard_map/while/body/eval_jaxpr/convert_element_type | solution.py:159
  572.4 5.3 fusion.168
  577.8 7.6 fusion.170
  597.9 5.9 bitcast_convert_fusion
  604.5 3.8 collective-permute-done.9
  611.1 4.6 fusion.86
  616.8 7.9 fusion.83
  624.7 4.3 copy.77
  632.2 25.2 %collective-permute-done.10 = bf16[1024,1024]{1,0:T(8,128)(2,1)} collective-permute-done((bf16[1024,1024]{1,0:T(8,128)(2,1)S(1)}, bf16[1024,1024]{1,0:T(8,128)(2,1)}, u32[]{:S(2)}, u32[]{:S(2)}) %collective-permute-start.10) | collective-permute-done | bytes 2097184 | tf_op jit(solution)/shard_map/ppermute | solution.py:39
  657.4 3.9 add_convert_fusion.2
  665.2 14.6 %reduce-scatter.15.cloned.1.call-done = bf16[128,256]{1,0:T(8,128)(2,1)} async-done(((bf16[1024,256]{1,0:T(8,128)(2,1)}), bf16[128,256]{1,0:T(8,128)(2,1)}) %reduce-scatter.15.cloned.1.call-update) | async-done | bytes 65552
  681.4 66.2 %reduce-scatter.13.cloned.1.call-done = bf16[128,768]{1,0:T(8,128)(2,1)} async-done(((bf16[1024,768]{1,0:T(8,128)(2,1)}), bf16[128,768]{1,0:T(8,128)(2,1)}) %reduce-scatter.13.cloned.1.call-update) | async-done | bytes 196624
  755.9 7.0 fusion.58
  763.1 34.7 %psum.7 = f32[7680]{0:T(1024)S(1)} all-reduce(f32[7680]{0:T(1024)S(1)} %constant_dynamic-update-slice_fusion), channel_id=1, replica_groups=mesh['dp'=8,'mp'=4] {'dp'}, use_global_device_ids=true, to_apply=%region_27.28 | all-reduce | flops 7680 | bytes 61440 | tf_op jit(solution)/shard_map/psum | solution.py:218
  798.4 12.3 %add_add_fusion.2 = f32[2048,1024]{1,0:T(8,128)} fusion(f32[2048,1024]{1,0:T(8,128)} %copy-done.9, bf16[2048,1024]{1,0:T(8,128)(2,1)} %param.19, f32[2048]{0:T(1024)S(1)} %negate_multiply_fusion.1, f32[2048]{0:T(1024)S(1)} %multiply_multiply_fusion.5, f32[1024]{0:T(1024)S(1)} %copy-done.45, f32[2048]{0:T(1024)S(1)} %copy-done.37, f32[2048]{0:T(1024)S(1)} %copy-done.35, ...), kind=kLoop, calls=%fused_computation.83 | loop fusion | flops 27262976 | bytes 25202688 | tf_op jit(solution)/shard_map/add | solution.py:196
  (280 shorter events, 138.1 us)
Async XLA Ops:
  7.2 177.3 %copy-start = (bf16[1024,1024]{1,0:T(8,128)(2,1)S(1)}, bf16[1024,1024]{1,0:T(8,128)(2,1)}, u32[]{:S(2)}) copy-start(bf16[1024,1024]{1,0:T(8,128)(2,1)} %param.28) | copy-start | bytes 6291460
  7.2 9.1 %copy-start.44 = (f32[1024]{0:T(1024)S(1)}, f32[1024]{0:T(1024)}, u32[]{:S(2)}) copy-start(f32[1024]{0:T(1024)} %param.30) | copy-start | bytes 12292
  7.2 9.1 %copy-start.51 = (f32[1024]{0:T(1024)S(1)}, f32[1024]{0:T(1024)}, u32[]{:S(2)}) copy-start(f32[1024]{0:T(1024)} %param.31) | copy-start | bytes 12292
  7.2 654.0 %reduce-scatter.17.cloned.1.call-start = ((), (), s32[]{:S(2)}) async-start(), calls=%async_computation.7 | async-start | bytes 2359296
  9.1 7.2 copy-start.2
  9.1 8.9 %copy-start.56 = (bf16[3,1024,256]{2,1,0:T(8,128)(2,1)S(1)}, bf16[3,1024,256]{2,1,0:T(8,128)(2,1)}, u32[]{:S(2)}) copy-start(bf16[3,1024,256]{2,1,0:T(8,128)(2,1)} %param.22) | copy-start | bytes 4718596
  96.9 9.9 %copy-start.6 = (bf16[2048,4,64]{0,2,1:T(8,128)(2,1)}, bf16[2048,4,64]{0,2,1:T(8,128)(2,1)S(1)}, u32[]{:S(2)}) copy-start(bf16[2048,4,64]{0,2,1:T(8,128)(2,1)S(1)} %get-tuple-element.562) | copy-start | bytes 3145732
  96.9 9.9 %copy-start.30 = (s32[2048]{0:T(1024)}, s32[2048]{0:T(1024)S(1)}, u32[]{:S(2)}) copy-start(s32[2048]{0:T(1024)S(1)} %get-tuple-element.585) | copy-start | bytes 24580
  96.9 9.8 %copy-start.39 = (s32[4,512]{1,0:T(4,128)}, s32[4,512]{1,0:T(4,128)S(1)}, u32[]{:S(2)}) copy-start(s32[4,512]{1,0:T(4,128)S(1)} %get-tuple-element.603) | copy-start | bytes 24580
  106.8 4.7 collective-permute-start
  114.7 58.2 %copy-start.38 = (f32[1024]{0:T(1024)S(1)}, f32[1024]{0:T(1024)}, u32[]{:S(2)}) copy-start(f32[1024]{0:T(1024)} %param.25) | copy-start | bytes 12292
  114.7 48.9 %collective-permute-start.1 = (bf16[1024,1024]{1,0:T(8,128)(2,1)S(1)}, bf16[1024,1024]{1,0:T(8,128)(2,1)S(1)}, u32[]{:S(2)}, u32[]{:S(2)}) collective-permute-start(bf16[1024,1024]{1,0:T(8,128)(2,1)S(1)} %add_convert_fusion.9), channel_id=1, source_target_pairs={{0,2},{1,3},{2,0},{3,1},{4,6},{5,7},{6,4},{7,5},{8,10},{9,11},{10,... | collective-permute-start | bytes 6291464 | tf_op jit(solution)/shard_map/ppermute | solution.py:39
  165.8 4.5 collective-permute-start.2
  165.8 7.0 copy-start.3
  184.5 25.6 %copy-start.21 = (f32[2048,1024]{1,0:T(8,128)}, f32[2048,1024]{1,0:T(8,128)S(1)}, u32[]{:S(2)}) copy-start(f32[2048,1024]{1,0:T(8,128)S(1)} %fusion.100) | copy-start | bytes 25165828
  220.1 10.9 %copy-start.23 = (bf16[2048,1024]{1,0:T(8,128)(2,1)S(1)}, bf16[2048,1024]{1,0:T(8,128)(2,1)}, u32[]{:S(2)}) copy-start(bf16[2048,1024]{1,0:T(8,128)(2,1)} %param.20) | copy-start | bytes 12582916
  220.1 10.9 %copy-start.28 = (bf16[2048,1024]{1,0:T(8,128)(2,1)S(1)}, bf16[2048,1024]{1,0:T(8,128)(2,1)}, u32[]{:S(2)}) copy-start(bf16[2048,1024]{1,0:T(8,128)(2,1)} %multiply_convert_fusion.1) | copy-start | bytes 12582916
  230.9 18.2 %collective-permute-start.6 = (bf16[1024,1024]{1,0:T(8,128)(2,1)}, bf16[1024,1024]{1,0:T(8,128)(2,1)}, u32[]{:S(2)}, u32[]{:S(2)}) collective-permute-start(bf16[1024,1024]{1,0:T(8,128)(2,1)} %constant_dynamic-slice_fusion.3), channel_id=1, source_target_pairs={{0,1},{1,0},{2,3},{3,2},{4,5},{5,4},{6,7},{7,6},{8,9},{9,8},{10,11... | collective-permute-start | bytes 6291464 | tf_op jit(solution)/shard_map/ppermute | solution.py:37
  240.8 422.4 %reduce-scatter.11.cloned.1.call-start = ((), (), s32[]{:S(2)}) async-start(), calls=%async_computation.4 | async-start | bytes 2359296 | tf_op jit(solution)/shard_map/reduce_scatter | solution.py:198
  240.9 8.2 %copy-start.27 = (bf16[2048,1024]{1,0:T(8,128)(2,1)S(1)}, bf16[2048,1024]{1,0:T(8,128)(2,1)}, u32[]{:S(2)}) copy-start(bf16[2048,1024]{1,0:T(8,128)(2,1)} %copy-done.26) | copy-start | bytes 12582916
  248.6 54.2 %copy-start.13 = (bf16[1024,1024]{1,0:T(8,128)(2,1)S(1)}, bf16[1024,1024]{1,0:T(8,128)(2,1)}, u32[]{:S(2)}) copy-start(bf16[1024,1024]{1,0:T(8,128)(2,1)} %copy-done.12) | copy-start | bytes 6291460
  248.7 5.2 collective-permute-start.3
  252.0 48.6 %collective-permute-start.7 = (bf16[1024,1024]{1,0:T(8,128)(2,1)S(1)}, bf16[1024,1024]{1,0:T(8,128)(2,1)S(1)}, u32[]{:S(2)}, u32[]{:S(2)}) collective-permute-start(bf16[1024,1024]{1,0:T(8,128)(2,1)S(1)} %add_convert_fusion.5), channel_id=1, source_target_pairs={{0,2},{1,3},{2,0},{3,1},{4,6},{5,7},{6,4},{7,5},{8,10},{9,11},{10,... | collective-permute-start | bytes 6291464 | tf_op jit(solution)/shard_map/ppermute | solution.py:39
  256.2 88.6 %collective-permute-start.4 = (bf16[1024,1024]{1,0:T(8,128)(2,1)}, bf16[1024,1024]{1,0:T(8,128)(2,1)}, u32[]{:S(2)}, u32[]{:S(2)}) collective-permute-start(bf16[1024,1024]{1,0:T(8,128)(2,1)} %add_convert_fusion.7), channel_id=1, source_target_pairs={{0,2},{1,3},{2,0},{3,1},{4,6},{5,7},{6,4},{7,5},{8,10},{9,11},{10,... | collective-permute-start | bytes 6291464 | tf_op jit(solution)/shard_map/ppermute | solution.py:39
  302.9 45.2 %collective-permute-start.8 = (bf16[1024,1024]{1,0:T(8,128)(2,1)}, bf16[1024,1024]{1,0:T(8,128)(2,1)}, u32[]{:S(2)}, u32[]{:S(2)}) collective-permute-start(bf16[1024,1024]{1,0:T(8,128)(2,1)} %add_convert_fusion.4), channel_id=1, source_target_pairs={{0,1},{1,0},{2,3},{3,2},{4,5},{5,4},{6,7},{7,6},{8,9},{9,8},{10,11... | collective-permute-start | bytes 6291464 | tf_op jit(solution)/shard_map/ppermute | solution.py:41
  314.0 365.8 %reduce-scatter.15.cloned.1.call-start = ((), (), s32[]{:S(2)}) async-start(), calls=%async_computation.6 | async-start | bytes 589824
  314.2 36.4 %copy-start.4 = (bf16[2048,1024]{1,0:T(8,128)(2,1)S(1)}, bf16[2048,1024]{1,0:T(8,128)(2,1)}, u32[]{:S(2)}) copy-start(bf16[2048,1024]{1,0:T(8,128)(2,1)} %param.19) | copy-start | bytes 12582916
  314.2 36.4 %copy-start.15 = (bf16[1024,1024]{1,0:T(8,128)(2,1)S(1)}, bf16[1024,1024]{1,0:T(8,128)(2,1)}, u32[]{:S(2)}) copy-start(bf16[1024,1024]{1,0:T(8,128)(2,1)} %copy-done.14) | copy-start | bytes 6291460
  347.9 18.7 %collective-permute-start.5 = (bf16[1024,1024]{1,0:T(8,128)(2,1)S(1)}, bf16[1024,1024]{1,0:T(8,128)(2,1)S(1)}, u32[]{:S(2)}, u32[]{:S(2)}) collective-permute-start(bf16[1024,1024]{1,0:T(8,128)(2,1)S(1)} %add_convert_fusion.6), channel_id=1, source_target_pairs={{0,1},{1,0},{2,3},{3,2},{4,5},{5,4},{6,7},{7,6},{8,9},{9,8},{10,11... | collective-permute-start | bytes 6291464 | tf_op jit(solution)/shard_map/ppermute | solution.py:41
  350.6 6.4 copy-start.43
  357.1 9.8 %copy-start.24 = (bf16[2048,1024]{1,0:T(8,128)(2,1)S(1)}, bf16[2048,1024]{1,0:T(8,128)(2,1)}, u32[]{:S(2)}) copy-start(bf16[2048,1024]{1,0:T(8,128)(2,1)} %param.20) | copy-start | bytes 12582916
  357.1 9.8 %copy-start.52 = (f32[1024]{0:T(1024)S(1)}, f32[1024]{0:T(1024)}, u32[]{:S(2)}) copy-start(f32[1024]{0:T(1024)} %param.29) | copy-start | bytes 12292
  366.9 15.1 %copy-start.29 = (bf16[256,1024]{1,0:T(8,128)(2,1)S(1)}, bf16[256,1024]{1,0:T(8,128)(2,1)}, u32[]{:S(2)}) copy-start(bf16[256,1024]{1,0:T(8,128)(2,1)} %param.24) | copy-start | bytes 1572868
  382.0 8.0 copy-start.7
  382.0 8.0 copy-start.31
  414.6 11.1 %copy-start.10 = (f32[2048,4,64]{0,2,1:T(8,128)S(1)}, f32[2048,4,64]{0,2,1:T(8,128)}, u32[]{:S(2)}) copy-start(f32[2048,4,64]{0,2,1:T(8,128)} %get-tuple-element.533) | copy-start | bytes 6291460 | tf_op jit(solution)/shard_map/while
  425.8 13.0 %copy-start.32 = (s32[2048]{0:T(1024)S(1)}, s32[2048]{0:T(1024)}, u32[]{:S(2)}) copy-start(s32[2048]{0:T(1024)} %get-tuple-element.599) | copy-start | bytes 24580 | tf_op jit(solution)/shard_map/while
  431.1 7.7 copy-start.11
  463.5 11.1 %copy-start.10 = (f32[2048,4,64]{0,2,1:T(8,128)S(1)}, f32[2048,4,64]{0,2,1:T(8,128)}, u32[]{:S(2)}) copy-start(f32[2048,4,64]{0,2,1:T(8,128)} %get-tuple-element.533) | copy-start | bytes 6291460 | tf_op jit(solution)/shard_map/while
  474.7 13.0 %copy-start.32 = (s32[2048]{0:T(1024)S(1)}, s32[2048]{0:T(1024)}, u32[]{:S(2)}) copy-start(s32[2048]{0:T(1024)} %get-tuple-element.599) | copy-start | bytes 24580 | tf_op jit(solution)/shard_map/while
  480.0 7.7 copy-start.11
  512.4 11.1 %copy-start.10 = (f32[2048,4,64]{0,2,1:T(8,128)S(1)}, f32[2048,4,64]{0,2,1:T(8,128)}, u32[]{:S(2)}) copy-start(f32[2048,4,64]{0,2,1:T(8,128)} %get-tuple-element.533) | copy-start | bytes 6291460 | tf_op jit(solution)/shard_map/while
  523.6 13.0 %copy-start.32 = (s32[2048]{0:T(1024)S(1)}, s32[2048]{0:T(1024)}, u32[]{:S(2)}) copy-start(s32[2048]{0:T(1024)} %get-tuple-element.599) | copy-start | bytes 24580 | tf_op jit(solution)/shard_map/while
  528.9 7.6 copy-start.11
  561.3 11.1 %copy-start.10 = (f32[2048,4,64]{0,2,1:T(8,128)S(1)}, f32[2048,4,64]{0,2,1:T(8,128)}, u32[]{:S(2)}) copy-start(f32[2048,4,64]{0,2,1:T(8,128)} %get-tuple-element.533) | copy-start | bytes 6291460 | tf_op jit(solution)/shard_map/while
  572.4 13.0 %copy-start.32 = (s32[2048]{0:T(1024)S(1)}, s32[2048]{0:T(1024)}, u32[]{:S(2)}) copy-start(s32[2048]{0:T(1024)} %get-tuple-element.599) | copy-start | bytes 24580 | tf_op jit(solution)/shard_map/while
  577.8 7.7 copy-start.11
  603.8 7.3 copy-start.20
  604.0 4.3 collective-permute-start.9
  609.3 48.1 %collective-permute-start.10 = (bf16[1024,1024]{1,0:T(8,128)(2,1)S(1)}, bf16[1024,1024]{1,0:T(8,128)(2,1)}, u32[]{:S(2)}, u32[]{:S(2)}) collective-permute-start(bf16[1024,1024]{1,0:T(8,128)(2,1)S(1)} %add_convert_fusion.3), channel_id=1, source_target_pairs={{0,2},{1,3},{2,0},{3,1},{4,6},{5,7},{6,4},{7,5},{8,10},{9,11},{10,... | collective-permute-start | bytes 6291464 | tf_op jit(solution)/shard_map/ppermute | solution.py:39
  616.8 130.9 %reduce-scatter.13.cloned.1.call-start = ((), (), s32[]{:S(2)}) async-start(), calls=%async_computation.5 | async-start | bytes 1769472
  632.2 119.6 %copy-start.35 = (f32[2048]{0:T(1024)S(1)}, f32[2048]{0:T(1024)}, u32[]{:S(2)}) copy-start(f32[2048]{0:T(1024)} %copy-done.34) | copy-start | bytes 24580
  632.2 119.6 %copy-start.45 = (f32[1024]{0:T(1024)S(1)}, f32[1024]{0:T(1024)}, u32[]{:S(2)}) copy-start(f32[1024]{0:T(1024)} %param.30) | copy-start | bytes 12292
  661.2 88.5 %collective-permute-start.11 = (bf16[1024,1024]{1,0:T(8,128)(2,1)}, bf16[1024,1024]{1,0:T(8,128)(2,1)S(1)}, u32[]{:S(2)}, u32[]{:S(2)}) collective-permute-start(bf16[1024,1024]{1,0:T(8,128)(2,1)} %add_convert_fusion.2), channel_id=1, source_target_pairs={{0,1},{1,0},{2,3},{3,2},{4,5},{5,4},{6,7},{7,6},{8,9},{9,8},{10,11... | collective-permute-start | bytes 6291464 | tf_op jit(solution)/shard_map/ppermute | solution.py:41
  749.8 6.1 copy-start.41
  749.8 6.1 copy-start.37
  751.8 11.1 %copy-start.16 = (bf16[1024,1024]{1,0:T(8,128)(2,1)}, bf16[1024,1024]{1,0:T(8,128)(2,1)S(1)}, u32[]{:S(2)}) copy-start(bf16[1024,1024]{1,0:T(8,128)(2,1)S(1)} %get-tuple-element.344) | copy-start | bytes 6291460
  751.8 11.1 %copy-start.17 = (bf16[1024,1024]{1,0:T(8,128)(2,1)}, bf16[1024,1024]{1,0:T(8,128)(2,1)S(1)}, u32[]{:S(2)}) copy-start(bf16[1024,1024]{1,0:T(8,128)(2,1)S(1)} %get-tuple-element.345) | copy-start | bytes 6291460
  752.6 10.4 %copy-start.48 = (f32[1024]{0:T(1024)S(1)}, f32[1024]{0:T(1024)}, u32[]{:S(2)}) copy-start(f32[1024]{0:T(1024)} %get-tuple-element.289) | copy-start | bytes 12292
  752.6 10.4 %copy-start.47 = (f32[1024]{0:T(1024)S(1)}, f32[1024]{0:T(1024)}, u32[]{:S(2)}) copy-start(f32[1024]{0:T(1024)} %get-tuple-element.293) | copy-start | bytes 12292
  752.6 10.4 %copy-start.50 = (f32[1024]{0:T(1024)S(1)}, f32[1024]{0:T(1024)}, u32[]{:S(2)}) copy-start(f32[1024]{0:T(1024)} %get-tuple-element.336) | copy-start | bytes 12292
  752.6 10.4 %copy-start.49 = (f32[1024]{0:T(1024)S(1)}, f32[1024]{0:T(1024)}, u32[]{:S(2)}) copy-start(f32[1024]{0:T(1024)} %get-tuple-element.343) | copy-start | bytes 12292
  752.6 10.4 %copy-start.53 = (f32[1024]{0:T(1024)S(1)}, f32[1024]{0:T(1024)}, u32[]{:S(2)}) copy-start(f32[1024]{0:T(1024)} %get-tuple-element.333) | copy-start | bytes 12292
  798.4 12.9 %copy-start.1 = (bf16[1024,1024]{1,0:T(8,128)(2,1)S(1)}, bf16[1024,1024]{1,0:T(8,128)(2,1)}, u32[]{:S(2)}) copy-start(bf16[1024,1024]{1,0:T(8,128)(2,1)} %param.28) | copy-start | bytes 6291460
  (25 other events, 96.6 us)
Sparse Core Ops, SparseCore 0:
  241.0 69.7 reduce-scatter.16
  314.3 70.0 reduce-scatter.10
  616.9 62.8 reduce-scatter.14
  683.1 64.5 reduce-scatter.12

commit v2 on v1

--- a/solution.py
+++ b/solution.py
@@ -3,10 +3,171 @@
 import jax
 import jax.numpy as jnp
 from jax import lax
+from jax.experimental import pallas as pl
+from jax.experimental.pallas import tpu as pltpu
 from jax.sharding import PartitionSpec as P
 
 HEAD = 64
 QBLOCK = 512
+TQ = 256
+TK = 256
+NEG = -1e30
+
+
+def _nt(a, b):
+    return lax.dot_general(a, b, (((1,), (1,)), ((), ())), preferred_element_type=jnp.float32)
+
+
+def _fwd_kernel(lo_ref, hi_ref, segc_ref, segr_ref, q_ref, k_ref, v_ref, o_ref, o32_ref, lse_ref):
+    rows = q_ref.shape[1]
+    scale = HEAD ** (-0.5)
+
+    def q_body(i, carry):
+        r0 = pl.multiple_of(i * TQ, TQ)
+        q = q_ref[0, pl.ds(r0, TQ), :]
+        sq = segc_ref[pl.ds(r0, TQ), :]
+        lo = lo_ref[i]
+        hi = hi_ref[i]
+
+        def scores(j):
+            c0 = pl.multiple_of(j * TK, TK)
+            s = _nt(q, k_ref[0, pl.ds(c0, TK), :]) * scale
+            same = sq == segr_ref[:, pl.ds(c0, TK)]
+            return jnp.where(same, s, NEG), c0
+
+        def stat_body(j, ml):
+            m, l = ml
+            s, _ = scores(j)
+            m_new = jnp.maximum(m, jnp.max(s, axis=-1, keepdims=True))
+            l = l * jnp.exp(m - m_new) + jnp.sum(jnp.exp(s - m_new), axis=-1, keepdims=True)
+            return m_new, l
+
+        m0 = jnp.full((TQ, 1), NEG, jnp.float32)
+        l0 = jnp.zeros((TQ, 1), jnp.float32)
+        m, l = lax.fori_loop(lo, hi, stat_body, (m0, l0))
+        inv_l = 1.0 / l
+
+        def acc_body(j, acc):
+            s, c0 = scores(j)
+            p = (jnp.exp(s - m) * inv_l).astype(jnp.bfloat16)
+            return acc + jnp.dot(p, v_ref[0, pl.ds(c0, TK), :], preferred_element_type=jnp.float32)
+
+        acc = lax.fori_loop(lo, hi, acc_body, jnp.zeros((TQ, HEAD), jnp.float32))
+        o_ref[0, pl.ds(r0, TQ), :] = acc.astype(o_ref.dtype)
+        o32_ref[0, pl.ds(r0, TQ), :] = acc
+        lse_ref[0, pl.ds(r0, TQ), :] = m + jnp.log(l)
+        return carry
+
+    lax.fori_loop(0, rows // TQ, q_body, 0)
+
+
+def _bwd_kernel(lo_ref, hi_ref, segc_ref, segr_ref, q_ref, k_ref, v_ref, do_ref, o32_ref, lse_ref,
+                dq_ref, dk_ref, dv_ref):
+    rows = q_ref.shape[1]
+    scale = HEAD ** (-0.5)
+    dk_ref[...] = jnp.zeros_like(dk_ref)
+    dv_ref[...] = jnp.zeros_like(dv_ref)
+
+    def q_body(i, carry):
+        r0 = pl.multiple_of(i * TQ, TQ)
+        q = q_ref[0, pl.ds(r0, TQ), :]
+        do = do_ref[0, pl.ds(r0, TQ), :]
+        sq = segc_ref[pl.ds(r0, TQ), :]
+        lse = lse_ref[0, pl.ds(r0, TQ), :]
+        dvec = jnp.sum(do.astype(jnp.float32) * o32_ref[0, pl.ds(r0, TQ), :], axis=-1, keepdims=True)
+
+        def kv_body(j, dq):
+            c0 = pl.multiple_of(j * TK, TK)
+            k = k_ref[0, pl.ds(c0, TK), :]
+            v = v_ref[0, pl.ds(c0, TK), :]
+            s = _nt(q, k) * scale
+            same = sq == segr_ref[:, pl.ds(c0, TK)]
+            s = jnp.where(same, s, NEG)
+            p = jnp.exp(s - lse)
+            dp = _nt(do, v)
+            ds = p * (dp - dvec)
+            dq = dq + jnp.dot(ds.astype(jnp.bfloat16), k, preferred_element_type=jnp.float32)
+            dk_ref[0, pl.ds(c0, TK), :] += jnp.dot(
+                ds.T.astype(jnp.bfloat16), q, preferred_element_type=jnp.float32)
+            dv_ref[0, pl.ds(c0, TK), :] += jnp.dot(
+                p.T.astype(jnp.bfloat16), do, preferred_element_type=jnp.float32)
+            return dq
+
+        dq = lax.fori_loop(lo_ref[i], hi_ref[i], kv_body, jnp.zeros((TQ, HEAD), jnp.float32))
+        dq_ref[0, pl.ds(r0, TQ), :] = dq * scale
+        return carry
+
+    lax.fori_loop(0, rows // TQ, q_body, 0)
+    dk_ref[...] = dk_ref[...] * scale
+
+
+def block_ranges(segments, item_lengths_row):
+    rows = segments.shape[0]
+    ends = jnp.cumsum(item_lengths_row.astype(jnp.int32))
+    starts = ends - item_lengths_row.astype(jnp.int32)
+    first = segments[0::TQ]
+    last = segments[TQ - 1::TQ]
+    n_items = item_lengths_row.shape[0]
+    key_lo = jnp.take(starts, jnp.clip(first, 0, n_items - 1))
+    key_hi = jnp.take(ends, jnp.clip(last, 0, n_items - 1))
+    lo = jnp.clip(key_lo // TK, 0, rows // TK)
+    hi = jnp.clip((key_hi + TK - 1) // TK, 0, rows // TK)
+    return lo.astype(jnp.int32), hi.astype(jnp.int32)
+
+
+def flash_forward(q, k, v, segments, lo, hi):
+    heads, rows, _ = q.shape
+    head_spec = pl.BlockSpec((1, rows, HEAD), lambda h, lo, hi: (h, 0, 0))
+    lse_spec = pl.BlockSpec((1, rows, 1), lambda h, lo, hi: (h, 0, 0))
+    col_spec = pl.BlockSpec((rows, 1), lambda h, lo, hi: (0, 0))
+    row_spec = pl.BlockSpec((1, rows), lambda h, lo, hi: (0, 0))
+    flops = int(heads * rows * rows * HEAD * 2 * 3 * 0.6)
+    return pl.pallas_call(
+        _fwd_kernel,
+        out_shape=(
+            jax.ShapeDtypeStruct((heads, rows, HEAD), jnp.bfloat16),
+            jax.ShapeDtypeStruct((heads, rows, HEAD), jnp.float32),
+            jax.ShapeDtypeStruct((heads, rows, 1), jnp.float32),
+        ),
+        grid_spec=pltpu.PrefetchScalarGridSpec(
+            num_scalar_prefetch=2,
+            grid=(heads,),
+            in_specs=[col_spec, row_spec, head_spec, head_spec, head_spec],
+            out_specs=[head_spec, head_spec, lse_spec],
+        ),
+        compiler_params=pltpu.CompilerParams(
+            dimension_semantics=("arbitrary",), vmem_limit_bytes=48 * 1024 * 1024),
+        cost_estimate=pl.CostEstimate(
+            flops=flops, transcendentals=int(heads * rows * rows * 0.6 * 2),
+            bytes_accessed=int(heads * rows * HEAD * (2 * 4 + 4) + heads * rows * 4)),
+        name="segment_flash_fwd",
+    )(lo, hi, segments.reshape(rows, 1), segments.reshape(1, rows), q, k, v)
+
+
+def flash_backward(q, k, v, do, o32, lse, segments, lo, hi):
+    heads, rows, _ = q.shape
+    head_spec = pl.BlockSpec((1, rows, HEAD), lambda h, lo, hi: (h, 0, 0))
+    lse_spec = pl.BlockSpec((1, rows, 1), lambda h, lo, hi: (h, 0, 0))
+    col_spec = pl.BlockSpec((rows, 1), lambda h, lo, hi: (0, 0))
+    row_spec = pl.BlockSpec((1, rows), lambda h, lo, hi: (0, 0))
+    flops = int(heads * rows * rows * HEAD * 2 * 5 * 0.6)
+    out = jax.ShapeDtypeStruct((heads, rows, HEAD), jnp.float32)
+    return pl.pallas_call(
+        _bwd_kernel,
+        out_shape=(out, out, out),
+        grid_spec=pltpu.PrefetchScalarGridSpec(
+            num_scalar_prefetch=2,
+            grid=(heads,),
+            in_specs=[col_spec, row_spec, head_spec, head_spec, head_spec, head_spec, head_spec, lse_spec],
+            out_specs=[head_spec, head_spec, head_spec],
+        ),
+        compiler_params=pltpu.CompilerParams(
+            dimension_semantics=("arbitrary",), vmem_limit_bytes=48 * 1024 * 1024),
+        cost_estimate=pl.CostEstimate(
+            flops=flops, transcendentals=int(heads * rows * rows * 0.6),
+            bytes_accessed=int(heads * rows * HEAD * (4 * 2 + 4 * 4) + heads * rows * 4)),
+        name="segment_flash_bwd",
+    )(lo, hi, segments.reshape(rows, 1), segments.reshape(1, rows), q, k, v, do, o32, lse)
 
 
 def normalize(values, gain, shift):
@@ -65,10 +226,7 @@
     row_count = tokens.shape[0]
     local_cols = w_qkv.shape[2]
     heads_here = local_cols // HEAD
-    blocks = row_count // QBLOCK
-    score_scale = HEAD ** (-0.5)
     segments = segment_ids(item_lengths[0], row_count)
-    seg_blocks = segments.reshape(blocks, QBLOCK)
     inputs = tokens.astype(jnp.float32)
     norm_one, norm_one_back = jax.vjp(normalize, inputs, ln1_gain, ln1_bias)
     normed_one = norm_one.astype(jnp.bfloat16)
@@ -81,35 +239,20 @@
     value_rows = (
         jnp.dot(normed_one, w_qkv[2], preferred_element_type=jnp.float32) + b_qv[1]
     ).astype(jnp.bfloat16)
-    key_heads = key_rows.reshape(row_count, heads_here, HEAD)
-    value_heads = value_rows.reshape(row_count, heads_here, HEAD)
-    query_blocks = queries.reshape(blocks, QBLOCK, heads_here, HEAD)
-
-    def block_scores(query_block, seg_block):
-        scores = (
-            jnp.einsum("qhd,khd->hqk", query_block, key_heads, preferred_element_type=jnp.float32)
-            * score_scale
-        )
-        same = seg_block[:, None] == segments[None, :]
-        return jnp.where(same[None], scores, -1e30)
-
-    def forward_block(pieces):
-        query_block, seg_block = pieces
-        scores = block_scores(query_block, seg_block)
-        row_max = jnp.max(scores, axis=-1, keepdims=True)
-        raised = jnp.exp(scores - row_max)
-        row_sum = jnp.sum(raised, axis=-1, keepdims=True)
-        probs = raised / row_sum
-        block_out = jnp.einsum(
-            "hqk,khd->qhd",
-            probs.astype(jnp.bfloat16),
-            value_heads,
-            preferred_element_type=jnp.float32,
-        )
-        return (block_out.astype(jnp.bfloat16), (row_max + jnp.log(row_sum))[..., 0])
-
-    out_blocks, log_norms = lax.map(forward_block, (query_blocks, seg_blocks))
-    attended = out_blocks.reshape(row_count, local_cols)
+    def to_heads(values):
+        return values.reshape(row_count, heads_here, HEAD).transpose(1, 0, 2)
+
+    def from_heads(values):
+        return values.transpose(1, 0, 2).reshape(row_count, local_cols)
+
+    lo_blocks, hi_blocks = block_ranges(segments, item_lengths[0])
+    query_heads = to_heads(queries)
+    key_heads = to_heads(key_rows)
+    value_heads = to_heads(value_rows)
+    out_heads, out_f32, log_norms = flash_forward(
+        query_heads, key_heads, value_heads, segments, lo_blocks, hi_blocks
+    )
+    attended = from_heads(out_heads)
     attention_sum = mp_allreduce(
         jnp.dot(attended, w_out, preferred_element_type=jnp.float32).astype(jnp.bfloat16), n_mp
     )
@@ -145,44 +288,13 @@
     d_attended = jnp.einsum(
         "td,cd->tc", d_middle_low, w_out, preferred_element_type=jnp.float32
     ).astype(jnp.bfloat16)
-    d_att_blocks = d_attended.reshape(blocks, QBLOCK, heads_here, HEAD)
-
-    def backward_block(running, pieces):
-        d_keys_acc, d_values_acc = running
-        query_block, seg_block, d_out_block, log_norm = pieces
-        scores = block_scores(query_block, seg_block)
-        probs = jnp.exp(scores - log_norm[..., None])
-        d_probs = jnp.einsum(
-            "qhd,khd->hqk", d_out_block, value_heads, preferred_element_type=jnp.float32
-        )
-        d_scores = probs * (d_probs - jnp.sum(probs * d_probs, axis=-1, keepdims=True))
-        d_scores_low = d_scores.astype(jnp.bfloat16)
-        d_query_block = (
-            jnp.einsum("hqk,khd->qhd", d_scores_low, key_heads, preferred_element_type=jnp.float32)
-            * score_scale
-        )
-        d_keys_acc = (
-            d_keys_acc
-            + jnp.einsum(
-                "hqk,qhd->khd", d_scores_low, query_block, preferred_element_type=jnp.float32
-            )
-            * score_scale
-        )
-        d_values_acc = d_values_acc + jnp.einsum(
-            "hqk,qhd->khd",
-            probs.astype(jnp.bfloat16),
-            d_out_block,
-            preferred_element_type=jnp.float32,
-        )
-        return ((d_keys_acc, d_values_acc), d_query_block)
-
-    zeros_acc = jnp.zeros((row_count, heads_here, HEAD), jnp.float32)
-    (d_keys, d_values), d_query_blocks = lax.scan(
-        backward_block, (zeros_acc, zeros_acc), (query_blocks, seg_blocks, d_att_blocks, log_norms)
-    )
-    d_queries = d_query_blocks.reshape(row_count, local_cols)
-    d_keys = d_keys.reshape(row_count, local_cols)
-    d_values = d_values.reshape(row_count, local_cols)
+    d_q_heads, d_k_heads, d_v_heads = flash_backward(
+        query_heads, key_heads, value_heads, to_heads(d_attended), out_f32, log_norms,
+        segments, lo_blocks, hi_blocks,
+    )
+    d_queries = from_heads(d_q_heads)
+    d_keys = from_heads(d_k_heads)
+    d_values = from_heads(d_v_heads)
     grad_b_qv = jnp.stack([jnp.sum(d_queries, axis=0), jnp.sum(d_values, axis=0)])
     stacked = jnp.stack([d_queries, d_keys, d_values]).astype(jnp.bfloat16)
     grad_w_qkv = jnp.einsum("td,stc->sdc", normed_one, stacked, preferred_element_type=jnp.float32)

time: 828 us -> 780 us (0.942)
  Pallas kernels: 0 us -> 187 us
  matrix products: 276 us -> 89.4 us
  other arithmetic: 182 us -> 125 us
    pallas_call x0 -> x2, Pallas kernels: none -> 187 us  [the longest x1 106 us: flash_forward(): pl.pallas_call(_fwd_kernel, out_shape=(jax.ShapeDtypeStruct((heads, rows,...]
    dot_general x28 -> x0, matrix products: 184 us -> none  [the longest x4 46 us: backward_block(): jnp.einsum('qhd,khd->hqk', d_out_block, value_heads, preferred_element_ty...]
    convert_element_type x4 -> x0, other arithmetic: 44.5 us -> none  [backward_block(): d_scores_low = d_scores.astype(jnp.bfloat16)]
    reduce_sum x4 -> x0, other arithmetic: 17.3 us -> none  [forward_block(): row_sum = jnp.sum(raised, axis=-1, keepdims=True)]
    unnamed x125 -> x113, local copies, waits for them, and re-layouts: 30.4 us -> 35.7 us
  transfers between devices with their start and end apart: 16 -> 16, of which waited for: 9 -> 9; matrix products, arithmetic and copies ran while one was open for 40% -> 18% of each run, Pallas kernels for 0% -> 11%
where the time goes in v2:
time: 780 us; the launch traced here: 770 us
  waiting for transfers between devices  245 us (31%)
  Pallas kernels  187 us (24%)
  other arithmetic  125 us (16%)
  matrix products  89.4 us (11%)
  local copies, waits for them, and re-layouts  66.5 us (9%)
  blocking collectives  34.8 us (4%)
  between operations  15.1 us (2%)
  starting transfers between devices  8.08 us (1%)
    ppermute x4, waiting for transfers between devices, mp_allreduce(): got_far = lax.ppermute(first, 'mp', [(k, k ^ 2) for k in range(4)])  149 us
    pallas_call x1, Pallas kernels, flash_forward(): pl.pallas_call(_fwd_kernel, out_shape=(jax.ShapeDtypeStruct((heads, rows,...  106 us
    unnamed x7, waiting for transfers between devices  82.7 us
    pallas_call x1, Pallas kernels, flash_backward(): pl.pallas_call(_bwd_kernel, out_shape=(out, out, out), grid_spec=pltpu.Pr...  81.3 us
    unnamed x113, local copies, waits for them, and re-layouts  35.7 us
    psum x1, blocking collectives, per_device(): packed = lax.psum(packed, 'dp')  34.8 us
    dot_general x1, matrix products, per_device(): jnp.einsum('td,fd->tf', cotangent, w_fc2, preferred_element_type=jnp.floa...  25.2 us
    reduce_sum x4, other arithmetic, normalize(): return centered * lax.rsqrt(spread + 1e-06) * gain + shift  25.2 us
  transfers between devices with their start and end apart: 16, of which 9 were waited for; matrix products, arithmetic and copies ran while one was open for 18% of the time, Pallas kernels for 11%

profile of v2, /device:TPU:0, one launch (start us, length us, event | category | flops | bytes accessed | tf_op | source)
XLA Modules:
  0.0 770.3 jit_solution(12872976795800310120)
XLA Ops:
  11.3 3.0 convert_reduce_fusion.2
  17.1 3.4 fusion.9
  20.6 2.3 convolution_convert_fusion.4
  22.9 2.3 fusion.28
  25.2 2.3 fusion.27
  27.5 2.7 copy.76
  30.2 2.7 copy.78
  32.9 2.7 copy.77
  37.2 105.6 %segment_flash_fwd.1 = (bf16[4,2048,64]{2,1,0:T(8,128)(2,1)S(1)}, f32[4,2048,64]{2,1,0:T(8,128)}, f32[4,2048,1]{2,1,0:T(8,128)}) custom-call(s32[8]{0:T(128)S(1)} %fusion.56.lo_ref, s32[8]{0:T(128)S(1)} %fusion.55.hi_ref, s32[2048,1]{1,0:T(8,128)S(1)} %copy.79.segc_ref, s32[1,2048]{1,0:T(1,128)S(1)} %bitcast.86, bf16[4,2048,64]{2,1,0:T(8,128)(2,1)S(1)} %bitcast.80, ...), custom_call_target="tpu_custom_call" | custom-call | flops 3865470464 | bytes 6324224 | tf_op jit(solution)/shard_map/segment_flash_fwd/pallas_call | solution.py:125
  144.2 2.7 copy.80
  146.9 2.6 convolution_convert_fusion
  149.5 2.0 copy-done.19
  153.5 4.1 collective-permute-done
  157.7 3.2 add_convert_fusion.9
  160.9 2.9 collective-permute-start.1
  163.8 45.9 %collective-permute-done.1 = bf16[1024,1024]{1,0:T(8,128)(2,1)S(1)} collective-permute-done((bf16[1024,1024]{1,0:T(8,128)(2,1)S(1)}, bf16[1024,1024]{1,0:T(8,128)(2,1)S(1)}, u32[]{:S(2)}, u32[]{:S(2)}) %collective-permute-start.1) | collective-permute-done | bytes 2097184 | tf_op jit(solution)/shard_map/ppermute | solution.py:200
  209.7 2.3 add_convert_fusion.8
  212.1 4.5 collective-permute-done.2
  216.6 2.5 broadcast_select_fusion.7
  220.7 3.5 multiply_reduce_fusion
  224.9 5.8 fusion.60
  230.8 25.2 %fusion.63 = (f32[1024]{0:T(1024)S(1)}, bf16[2048,1024]{1,0:T(8,128)(2,1)}, f32[2048,1024]{1,0:T(8,128)}) fusion(f32[2048,1024]{1,0:T(8,128)S(1)} %fusion.60, f32[1024]{0:T(1024)S(1)} %copy-done.43, bf16[2048,1024]{1,0:T(8,128)(2,1)S(1)} %copy-done.22, bf16[1024,1024]{1,0:T(8,128)(2,1)S(1)} %copy-done), kind=kOutput, calls=%fused_computation.155 | convolution fusion | flops 4450155520 | bytes 27271168 | tf_op jit(solution)/shard_map/td,fd->tf/dot_general | solution.py:272
  256.0 10.1 %multiply_convert_fusion = bf16[2048,1024]{1,0:T(8,128)(2,1)} fusion(f32[2048,1024]{1,0:T(8,128)} %get-tuple-element.105, f32[2048,1024]{1,0:T(8,128)} %copy-done.21, f32[1024]{0:T(1024)S(1)} %copy-done.43), kind=kLoop, calls=%fused_computation.37 | loop fusion | flops 8388608 | bytes 20975616 | tf_op jit(solution)/shard_map/convert_element_type | solution.py:264
  266.1 7.1 convolution_convert_fusion.1
  273.2 2.0 copy-done.25
  278.2 5.8 convolution_convert_fusion.5
  284.0 3.9 copy.96
  288.0 7.4 convolution_convert_fusion.2
  297.5 2.6 add_convert_fusion.5
  301.9 2.4 add_convert_fusion.7
  304.5 44.1 %collective-permute-done.7 = bf16[1024,1024]{1,0:T(8,128)(2,1)S(1)} collective-permute-done((bf16[1024,1024]{1,0:T(8,128)(2,1)S(1)}, bf16[1024,1024]{1,0:T(8,128)(2,1)S(1)}, u32[]{:S(2)}, u32[]{:S(2)}) %collective-permute-start.7) | collective-permute-done | bytes 2097184 | tf_op jit(solution)/shard_map/ppermute | solution.py:200
  348.7 2.3 add_convert_fusion.4
  351.0 7.5 fusion.35
  358.7 34.1 %collective-permute-done.4 = bf16[1024,1024]{1,0:T(8,128)(2,1)} collective-permute-done((bf16[1024,1024]{1,0:T(8,128)(2,1)}, bf16[1024,1024]{1,0:T(8,128)(2,1)}, u32[]{:S(2)}, u32[]{:S(2)}) %collective-permute-start.4) | collective-permute-done | bytes 2097184 | tf_op jit(solution)/shard_map/ppermute | solution.py:200
  392.9 3.2 add_convert_fusion.6
  396.2 2.7 broadcast_select_fusion.3
  400.9 6.3 fusion.10
  407.2 8.7 %fusion.15 = (f32[1024]{0:T(1024)S(1)}, f32[2048]{0:T(1024)S(1)}, f32[1024]{0:T(1024)S(1)}) fusion(f32[2048]{0:T(1024)S(1)} %fusion.54, bf16[1024,1024]{1,0:T(8,128)(2,1)S(1)} %get-tuple-element.113, bf16[1024,1024]{1,0:T(8,128)(2,1)S(1)} %get-tuple-element.112, f32[2048]{0:T(1024)S(1)} %broadcast_multiply_fusion, f32[1024]{0:T(1024)S(1)} %copy-done.33, ...), kind=kLoop, calls=%fused_computation.31 | loop fusion | flops 46133248 | bytes 12632064 | tf_op jit(solution)/shard_map/transpose(jvp())/reduce_sum | solution.py:177
  416.7 12.2 %fusion.65 = (f32[1024]{0:T(1024)S(1)}, f32[2048,1024]{1,0:T(8,128)S(1)}, bf16[2048,1024]{1,0:T(8,128)(2,1)}, f32[1024]{0:T(1024)S(1)}) fusion(f32[2048]{0:T(1024)S(1)} %negate_multiply_fusion.2, f32[2048]{0:T(1024)S(1)} %multiply_multiply_fusion.6, f32[2048]{0:T(1024)S(1)} %broadcast_multiply_fusion, f32[1024]{0:T(1024)S(1)} %copy-done.33, ...), kind=kLoop, calls=%fused_computation.156 | loop fusion | flops 60815360 | bytes 33607680 | tf_op jit(solution)/shard_map/reduce_sum | solution.py:285
  428.9 2.7 convolution_convert_fusion.3
  432.6 2.8 copy.81
  438.6 81.3 %segment_flash_bwd.1 = (f32[4,2048,64]{2,1,0:T(8,128)}, f32[4,2048,64]{2,1,0:T(8,128)}, f32[4,2048,64]{2,1,0:T(8,128)}) custom-call(s32[8]{0:T(128)S(1)} %fusion.56.lo_ref, s32[8]{0:T(128)S(1)} %fusion.55.hi_ref, s32[2048,1]{1,0:T(8,128)S(1)} %copy.79.segc_ref, s32[1,2048]{1,0:T(1,128)S(1)} %bitcast.87, bf16[4,2048,64]{2,1,0:T(8,128)(2,1)S(1)} %bitcast.81, ...), custom_call_target="tpu_custom_call" | custom-call | flops 6442450944 | bytes 12615680 | tf_op jit(solution)/shard_map/segment_flash_bwd/pallas_call | solution.py:155
  519.9 3.8 convert_bitcast_fusion
  523.7 1.9 copy.84
  527.0 3.8 bitcast_convert_fusion.2
  534.0 3.8 bitcast_convert_fusion.1
  541.2 5.8 bitcast_convert_fusion
  547.3 4.1 collective-permute-done.9
  551.4 2.3 add_convert_fusion.3
  555.4 4.7 fusion.44
  561.2 7.8 %fusion.41 = bf16[3,1024,256]{1,2,0:T(8,128)(2,1)} fusion(bf16[2048,1024]{1,0:T(8,128)(2,1)} %copy-done.24, bf16[1,2048,256]{2,1,0:T(8,128)(2,1)} %copy.88, bf16[1,2048,256]{2,1,0:T(8,128)(2,1)} %copy.87, bf16[1,2048,256]{2,1,0:T(8,128)(2,1)} %copy.86), kind=kOutput, calls=%fused_computation.101 | convolution fusion | flops 3225157632 | bytes 8912896 | tf_op jit(solution)/shard_map/td,stc->sdc/dot_general | solution.py:300
  569.0 4.4 copy.92
  573.4 3.1 copy.98
  576.6 25.1 %collective-permute-done.10 = bf16[1024,1024]{1,0:T(8,128)(2,1)} collective-permute-done((bf16[1024,1024]{1,0:T(8,128)(2,1)}, bf16[1024,1024]{1,0:T(8,128)(2,1)}, u32[]{:S(2)}, u32[]{:S(2)}) %collective-permute-start.10) | collective-permute-done | bytes 2097184 | tf_op jit(solution)/shard_map/ppermute | solution.py:200
  601.7 4.5 add_convert_fusion.2
  610.0 2.5 bitcast_reduce_fusion.1
  612.5 2.5 bitcast_reduce_fusion
  615.1 16.2 %reduce-scatter.15.cloned.1.call-done = bf16[128,256]{1,0:T(8,128)(2,1)} async-done(((bf16[1024,256]{1,0:T(8,128)(2,1)}), bf16[128,256]{1,0:T(8,128)(2,1)}) %reduce-scatter.15.cloned.1.call-update) | async-done | bytes 65552
  632.9 66.4 %reduce-scatter.13.cloned.1.call-done = bf16[128,768]{1,0:T(8,128)(2,1)} async-done(((bf16[1024,768]{1,0:T(8,128)(2,1)}), bf16[128,768]{1,0:T(8,128)(2,1)}) %reduce-scatter.13.cloned.1.call-update) | async-done | bytes 196624
  701.5 2.6 broadcast_select_fusion.1
  704.9 3.2 fusion.12
  708.2 7.0 fusion.16
  715.2 34.8 %psum.7 = f32[7680]{0:T(1024)S(1)} all-reduce(f32[7680]{0:T(1024)S(1)} %constant_dynamic-update-slice_fusion), channel_id=1, replica_groups=mesh['dp'=8,'mp'=4] {'dp'}, use_global_device_ids=true, to_apply=%region_20.22 | all-reduce | flops 7680 | bytes 61440 | tf_op jit(solution)/shard_map/psum | solution.py:330
  750.6 12.1 %add_add_fusion.2 = f32[2048,1024]{1,0:T(8,128)} fusion(f32[2048,1024]{1,0:T(8,128)} %copy-done.10, bf16[2048,1024]{1,0:T(8,128)(2,1)} %param.17, f32[2048]{0:T(1024)S(1)} %negate_multiply_fusion.1, f32[2048]{0:T(1024)S(1)} %multiply_multiply_fusion.5, f32[1024]{0:T(1024)S(1)} %copy-done.39, f32[2048]{0:T(1024)S(1)} %copy-done.32, f32[2048]{0:T(1024)S(1)} %copy-done.30, ...), kind=kLoop, calls=%fused_computation.34 | loop fusion | flops 27262976 | bytes 25202688 | tf_op jit(solution)/shard_map/add | solution.py:308
  (178 shorter events, 49.1 us)
Async XLA Ops:
  7.2 223.6 %copy-start = (bf16[1024,1024]{1,0:T(8,128)(2,1)S(1)}, bf16[1024,1024]{1,0:T(8,128)(2,1)}, u32[]{:S(2)}) copy-start(bf16[1024,1024]{1,0:T(8,128)(2,1)} %param.26) | copy-start | bytes 6291460
  7.2 599.0 %reduce-scatter.17.cloned.1.call-start = ((), (), s32[]{:S(2)}) async-start(), calls=%async_computation.7 | async-start | bytes 2359296
  11.3 3.5 copy-start.5
  11.3 5.8 copy-start.38
  11.3 5.8 copy-start.41
  14.7 5.8 copy-start.29
  16.1 0.6 copy-start.34
  16.7 3.8 copy-start.31
  17.1 3.4 copy-start.45
  20.5 4.6 copy-start.24
  35.7 1.6 copy-start.1
  142.9 1.3 copy-start.4
  149.5 2.0 copy-start.19
  153.0 4.6 collective-permute-start
  160.9 48.9 %collective-permute-start.1 = (bf16[1024,1024]{1,0:T(8,128)(2,1)S(1)}, bf16[1024,1024]{1,0:T(8,128)(2,1)S(1)}, u32[]{:S(2)}, u32[]{:S(2)}) collective-permute-start(bf16[1024,1024]{1,0:T(8,128)(2,1)S(1)} %add_convert_fusion.9), channel_id=1, source_target_pairs={{0,2},{1,3},{2,0},{3,1},{4,6},{5,7},{6,4},{7,5},{8,10},{9,11},{10,... | collective-permute-start | bytes 6291464 | tf_op jit(solution)/shard_map/ppermute | solution.py:200
  212.1 4.5 collective-permute-start.2
  212.1 7.0 copy-start.6
  212.1 7.0 copy-start.33
  219.1 5.8 copy-start.11
  219.1 5.8 copy-start.14
  220.7 4.2 copy-start.40
  220.7 4.2 copy-start.44
  220.7 4.2 copy-start.46
  224.2 0.6 copy-start.36
  224.9 5.9 copy-start.22
  224.9 5.9 copy-start.43
  230.8 25.2 %copy-start.21 = (f32[2048,1024]{1,0:T(8,128)}, f32[2048,1024]{1,0:T(8,128)S(1)}, u32[]{:S(2)}) copy-start(f32[2048,1024]{1,0:T(8,128)S(1)} %fusion.60) | copy-start | bytes 25165828
  266.1 10.8 %copy-start.27 = (bf16[2048,1024]{1,0:T(8,128)(2,1)S(1)}, bf16[2048,1024]{1,0:T(8,128)(2,1)}, u32[]{:S(2)}) copy-start(bf16[2048,1024]{1,0:T(8,128)(2,1)} %multiply_convert_fusion) | copy-start | bytes 12582916
  273.2 2.0 copy-start.25
  275.2 2.9 copy-start.23
  276.7 19.0 %collective-permute-start.6 = (bf16[1024,1024]{1,0:T(8,128)(2,1)}, bf16[1024,1024]{1,0:T(8,128)(2,1)}, u32[]{:S(2)}, u32[]{:S(2)}) collective-permute-start(bf16[1024,1024]{1,0:T(8,128)(2,1)} %constant_dynamic-slice_fusion.1), channel_id=1, source_target_pairs={{0,1},{1,0},{2,3},{3,2},{4,5},{5,4},{6,7},{7,6},{8,9},{9,8},{10,11... | collective-permute-start | bytes 6291464 | tf_op jit(solution)/shard_map/ppermute | solution.py:198
  287.9 320.2 %reduce-scatter.11.cloned.1.call-start = ((), (), s32[]{:S(2)}) async-start(), calls=%async_computation.4 | async-start | bytes 2359296 | tf_op jit(solution)/shard_map/reduce_scatter | solution.py:310
  295.3 2.2 copy-start.26
  295.5 6.3 collective-permute-start.3
  300.1 48.6 %collective-permute-start.7 = (bf16[1024,1024]{1,0:T(8,128)(2,1)S(1)}, bf16[1024,1024]{1,0:T(8,128)(2,1)S(1)}, u32[]{:S(2)}, u32[]{:S(2)}) collective-permute-start(bf16[1024,1024]{1,0:T(8,128)(2,1)S(1)} %add_convert_fusion.5), channel_id=1, source_target_pairs={{0,2},{1,3},{2,0},{3,1},{4,6},{5,7},{6,4},{7,5},{8,10},{9,11},{10,... | collective-permute-start | bytes 6291464 | tf_op jit(solution)/shard_map/ppermute | solution.py:200
  301.9 49.1 %copy-start.15 = (bf16[1024,1024]{1,0:T(8,128)(2,1)S(1)}, bf16[1024,1024]{1,0:T(8,128)(2,1)}, u32[]{:S(2)}) copy-start(bf16[1024,1024]{1,0:T(8,128)(2,1)} %copy-done.14) | copy-start | bytes 6291460
  301.9 49.1 %copy-start.47 = (bf16[2048,1024]{1,0:T(8,128)(2,1)S(1)}, bf16[2048,1024]{1,0:T(8,128)(2,1)}, u32[]{:S(2)}) copy-start(bf16[2048,1024]{1,0:T(8,128)(2,1)} %get-tuple-element.104) | copy-start | bytes 12582916
  304.2 46.8 %copy-start.7 = (bf16[2048,1024]{1,0:T(8,128)(2,1)S(1)}, bf16[2048,1024]{1,0:T(8,128)(2,1)}, u32[]{:S(2)}) copy-start(bf16[2048,1024]{1,0:T(8,128)(2,1)} %param.17) | copy-start | bytes 12582916
  304.2 46.8 %copy-start.12 = (bf16[1024,1024]{1,0:T(8,128)(2,1)S(1)}, bf16[1024,1024]{1,0:T(8,128)(2,1)}, u32[]{:S(2)}) copy-start(bf16[1024,1024]{1,0:T(8,128)(2,1)} %copy-done.11) | copy-start | bytes 6291460
  304.2 88.6 %collective-permute-start.4 = (bf16[1024,1024]{1,0:T(8,128)(2,1)}, bf16[1024,1024]{1,0:T(8,128)(2,1)}, u32[]{:S(2)}, u32[]{:S(2)}) collective-permute-start(bf16[1024,1024]{1,0:T(8,128)(2,1)} %add_convert_fusion.7), channel_id=1, source_target_pairs={{0,2},{1,3},{2,0},{3,1},{4,6},{5,7},{6,4},{7,5},{8,10},{9,11},{10,... | collective-permute-start | bytes 6291464 | tf_op jit(solution)/shard_map/ppermute | solution.py:200
  351.0 45.2 %collective-permute-start.8 = (bf16[1024,1024]{1,0:T(8,128)(2,1)}, bf16[1024,1024]{1,0:T(8,128)(2,1)}, u32[]{:S(2)}, u32[]{:S(2)}) collective-permute-start(bf16[1024,1024]{1,0:T(8,128)(2,1)} %add_convert_fusion.4), channel_id=1, source_target_pairs={{0,1},{1,0},{2,3},{3,2},{4,5},{5,4},{6,7},{7,6},{8,9},{9,8},{10,11... | collective-permute-start | bytes 6291464 | tf_op jit(solution)/shard_map/ppermute | solution.py:202
  358.5 272.8 %reduce-scatter.15.cloned.1.call-start = ((), (), s32[]{:S(2)}) async-start(), calls=%async_computation.6 | async-start | bytes 589824
  396.1 3.5 copy-start.8
  396.1 4.2 copy-start.13
  396.1 4.8 copy-start.16
  396.1 19.9 %collective-permute-start.5 = (bf16[1024,1024]{1,0:T(8,128)(2,1)S(1)}, bf16[1024,1024]{1,0:T(8,128)(2,1)S(1)}, u32[]{:S(2)}, u32[]{:S(2)}) collective-permute-start(bf16[1024,1024]{1,0:T(8,128)(2,1)S(1)} %add_convert_fusion.6), channel_id=1, source_target_pairs={{0,1},{1,0},{2,3},{3,2},{4,5},{5,4},{6,7},{7,6},{8,9},{9,8},{10,11... | collective-permute-start | bytes 6291464 | tf_op jit(solution)/shard_map/ppermute | solution.py:202
  400.9 6.3 copy-start.37
  416.0 0.7 copy-start.42
  416.7 12.2 %copy-start.28 = (bf16[256,1024]{1,0:T(8,128)(2,1)S(1)}, bf16[256,1024]{1,0:T(8,128)(2,1)}, u32[]{:S(2)}) copy-start(bf16[256,1024]{1,0:T(8,128)(2,1)} %param.22) | copy-start | bytes 1572868
  428.9 3.7 copy-start.10
  435.4 1.6 copy-start.2
  437.0 1.6 copy-start.3
  547.2 8.2 %copy-start.20 = (bf16[2048,4,64]{0,2,1:T(8,128)(2,1)S(1)}, bf16[2048,4,64]{0,2,1:T(8,128)(2,1)}, u32[]{:S(2)}) copy-start(bf16[2048,4,64]{0,2,1:T(8,128)(2,1)} %copy.80) | copy-start | bytes 3145732
  547.2 4.2 collective-permute-start.9
  553.7 48.0 %collective-permute-start.10 = (bf16[1024,1024]{1,0:T(8,128)(2,1)}, bf16[1024,1024]{1,0:T(8,128)(2,1)}, u32[]{:S(2)}, u32[]{:S(2)}) collective-permute-start(bf16[1024,1024]{1,0:T(8,128)(2,1)} %add_convert_fusion.3), channel_id=1, source_target_pairs={{0,2},{1,3},{2,0},{3,1},{4,6},{5,7},{6,4},{7,5},{8,10},{9,11},{10,... | collective-permute-start | bytes 6291464 | tf_op jit(solution)/shard_map/ppermute | solution.py:200
  561.1 138.2 %reduce-scatter.13.cloned.1.call-start = ((), (), s32[]{:S(2)}) async-start(), calls=%async_computation.5 | async-start | bytes 1769472
  606.2 95.3 %collective-permute-start.11 = (bf16[1024,1024]{1,0:T(8,128)(2,1)}, bf16[1024,1024]{1,0:T(8,128)(2,1)}, u32[]{:S(2)}, u32[]{:S(2)}) collective-permute-start(bf16[1024,1024]{1,0:T(8,128)(2,1)} %add_convert_fusion.2), channel_id=1, source_target_pairs={{0,1},{1,0},{2,3},{3,2},{4,5},{5,4},{6,7},{7,6},{8,9},{9,8},{10,11... | collective-permute-start | bytes 6291464 | tf_op jit(solution)/shard_map/ppermute | solution.py:202
  701.5 3.4 copy-start.9
  701.5 3.4 copy-start.30
  701.5 3.5 copy-start.39
  704.1 4.0 copy-start.17
  704.1 4.0 copy-start.18
  704.9 3.2 copy-start.35
  704.9 3.2 copy-start.32
Sparse Core Ops, SparseCore 0:
  288.0 72.5 reduce-scatter.16
  364.2 67.7 reduce-scatter.10
  561.3 69.9 reduce-scatter.14
  634.6 64.7 reduce-scatter.12

commit v3 on v2

--- a/solution.py
+++ b/solution.py
@@ -18,6 +18,10 @@
     return lax.dot_general(a, b, (((1,), (1,)), ((), ())), preferred_element_type=jnp.float32)
 
 
+def _lanes(values, width):
+    return jnp.tile(values, (1, width // 128))
+
+
 def _fwd_kernel(lo_ref, hi_ref, segc_ref, segr_ref, q_ref, k_ref, v_ref, o_ref, o32_ref, lse_ref):
     rows = q_ref.shape[1]
     scale = HEAD ** (-0.5)
@@ -26,36 +30,30 @@
         r0 = pl.multiple_of(i * TQ, TQ)
         q = q_ref[0, pl.ds(r0, TQ), :]
         sq = segc_ref[pl.ds(r0, TQ), :]
-        lo = lo_ref[i]
-        hi = hi_ref[i]
-
-        def scores(j):
+
+        def kv_body(j, state):
+            m, l, acc = state
             c0 = pl.multiple_of(j * TK, TK)
             s = _nt(q, k_ref[0, pl.ds(c0, TK), :]) * scale
             same = sq == segr_ref[:, pl.ds(c0, TK)]
-            return jnp.where(same, s, NEG), c0
-
-        def stat_body(j, ml):
-            m, l = ml
-            s, _ = scores(j)
+            s = jnp.where(same, s, NEG)
             m_new = jnp.maximum(m, jnp.max(s, axis=-1, keepdims=True))
-            l = l * jnp.exp(m - m_new) + jnp.sum(jnp.exp(s - m_new), axis=-1, keepdims=True)
-            return m_new, l
-
-        m0 = jnp.full((TQ, 1), NEG, jnp.float32)
-        l0 = jnp.zeros((TQ, 1), jnp.float32)
-        m, l = lax.fori_loop(lo, hi, stat_body, (m0, l0))
-        inv_l = 1.0 / l
-
-        def acc_body(j, acc):
-            s, c0 = scores(j)
-            p = (jnp.exp(s - m) * inv_l).astype(jnp.bfloat16)
-            return acc + jnp.dot(p, v_ref[0, pl.ds(c0, TK), :], preferred_element_type=jnp.float32)
-
-        acc = lax.fori_loop(lo, hi, acc_body, jnp.zeros((TQ, HEAD), jnp.float32))
-        o_ref[0, pl.ds(r0, TQ), :] = acc.astype(o_ref.dtype)
-        o32_ref[0, pl.ds(r0, TQ), :] = acc
-        lse_ref[0, pl.ds(r0, TQ), :] = m + jnp.log(l)
+            p = jnp.exp(s - _lanes(m_new, TK))
+            alpha = jnp.exp(m - m_new)
+            l = alpha * l + jnp.sum(p, axis=-1, keepdims=True)
+            pv = jnp.dot(p.astype(jnp.bfloat16), v_ref[0, pl.ds(c0, TK), :],
+                         preferred_element_type=jnp.float32)
+            acc = alpha[:, :HEAD] * acc + pv
+            return m_new, l, acc
+
+        m0 = jnp.full((TQ, 128), NEG, jnp.float32)
+        l0 = jnp.zeros((TQ, 128), jnp.float32)
+        acc0 = jnp.zeros((TQ, HEAD), jnp.float32)
+        m, l, acc = lax.fori_loop(lo_ref[i], hi_ref[i], kv_body, (m0, l0, acc0))
+        out = acc / l[:, :HEAD]
+        o_ref[0, pl.ds(r0, TQ), :] = out.astype(o_ref.dtype)
+        o32_ref[0, pl.ds(r0, TQ), :] = out
+        lse_ref[0, pl.ds(r0, TQ), :] = (m + jnp.log(l))[:, :1]
         return carry
 
     lax.fori_loop(0, rows // TQ, q_body, 0)
@@ -73,8 +71,9 @@
         q = q_ref[0, pl.ds(r0, TQ), :]
         do = do_ref[0, pl.ds(r0, TQ), :]
         sq = segc_ref[pl.ds(r0, TQ), :]
-        lse = lse_ref[0, pl.ds(r0, TQ), :]
+        lse = _lanes(jnp.broadcast_to(lse_ref[0, pl.ds(r0, TQ), :], (TQ, 128)), TK)
         dvec = jnp.sum(do.astype(jnp.float32) * o32_ref[0, pl.ds(r0, TQ), :], axis=-1, keepdims=True)
+        dvec = _lanes(jnp.broadcast_to(dvec, (TQ, 128)), TK)
 
         def kv_body(j, dq):
             c0 = pl.multiple_of(j * TK, TK)

time: 780 us -> 748 us (0.959)
  Pallas kernels: 187 us -> 156 us
    pallas_call x1, Pallas kernels: 106 us -> 74.3 us  [flash_forward(): pl.pallas_call(_fwd_kernel, out_shape=(jax.ShapeDtypeStruct((heads, rows,...]
  transfers between devices with their start and end apart: 16 -> 16, of which waited for: 9 -> 9; matrix products, arithmetic and copies ran while one was open for 18% -> 19% of each run, Pallas kernels for 11% -> 11%
where the time goes in v3:
time: 748 us; the launch traced here: 738 us
  waiting for transfers between devices  243 us (32%)
  Pallas kernels  156 us (21%)
  other arithmetic  125 us (17%)
  matrix products  89.4 us (12%)
  local copies, waits for them, and re-layouts  66.5 us (9%)
  blocking collectives  34.8 us (5%)
  between operations  15.1 us (2%)
  starting transfers between devices  8.13 us (1%)
    ppermute x4, waiting for transfers between devices, mp_allreduce(): got_far = lax.ppermute(first, 'mp', [(k, k ^ 2) for k in range(4)])  149 us
    pallas_call x1, Pallas kernels, flash_backward(): pl.pallas_call(_bwd_kernel, out_shape=(out, out, out), grid_spec=pltpu.Pr...  82.1 us
    unnamed x7, waiting for transfers between devices  80.6 us
    pallas_call x1, Pallas kernels, flash_forward(): pl.pallas_call(_fwd_kernel, out_shape=(jax.ShapeDtypeStruct((heads, rows,...  74.3 us
    unnamed x113, local copies, waits for them, and re-layouts  35.7 us
    psum x1, blocking collectives, per_device(): packed = lax.psum(packed, 'dp')  34.8 us
    reduce_sum x4, other arithmetic, normalize(): return centered * lax.rsqrt(spread + 1e-06) * gain + shift  25.2 us
    dot_general x1, matrix products, per_device(): jnp.einsum('td,fd->tf', cotangent, w_fc2, preferred_element_type=jnp.floa...  25.2 us
  transfers between devices with their start and end apart: 16, of which 9 were waited for; matrix products, arithmetic and copies ran while one was open for 19% of the time, Pallas kernels for 11%

profile of v3, /device:TPU:0, one launch (start us, length us, event | category | flops | bytes accessed | tf_op | source)
XLA Modules:
  0.0 737.7 jit_solution(18415969837730829654)
XLA Ops:
  11.3 3.0 convert_reduce_fusion.2
  17.1 3.4 fusion.9
  20.6 2.3 convolution_convert_fusion.4
  22.9 2.3 fusion.28
  25.2 2.3 fusion.27
  27.5 2.7 copy.76
  30.2 2.7 copy.78
  32.9 2.7 copy.77
  37.2 74.3 %segment_flash_fwd.1 = (bf16[4,2048,64]{2,1,0:T(8,128)(2,1)S(1)}, f32[4,2048,64]{2,1,0:T(8,128)}, f32[4,2048,1]{2,1,0:T(8,128)}) custom-call(s32[8]{0:T(128)S(1)} %fusion.56.lo_ref, s32[8]{0:T(128)S(1)} %fusion.55.hi_ref, s32[2048,1]{1,0:T(8,128)S(1)} %copy.79.segc_ref, s32[1,2048]{1,0:T(1,128)S(1)} %bitcast.86, bf16[4,2048,64]{2,1,0:T(8,128)(2,1)S(1)} %bitcast.80, ...), custom_call_target="tpu_custom_call" | custom-call | flops 3865470464 | bytes 6324224 | tf_op jit(solution)/shard_map/segment_flash_fwd/pallas_call | solution.py:124
  112.9 2.7 copy.80
  115.6 2.6 convolution_convert_fusion
  118.2 2.0 copy-done.19
  122.2 4.1 collective-permute-done
  126.3 3.2 add_convert_fusion.9
  129.5 2.9 collective-permute-start.1
  132.5 45.9 %collective-permute-done.1 = bf16[1024,1024]{1,0:T(8,128)(2,1)S(1)} collective-permute-done((bf16[1024,1024]{1,0:T(8,128)(2,1)S(1)}, bf16[1024,1024]{1,0:T(8,128)(2,1)S(1)}, u32[]{:S(2)}, u32[]{:S(2)}) %collective-permute-start.1) | collective-permute-done | bytes 2097184 | tf_op jit(solution)/shard_map/ppermute | solution.py:199
  178.4 2.3 add_convert_fusion.8
  180.8 4.5 collective-permute-done.2
  185.2 2.5 broadcast_select_fusion.7
  189.4 3.5 multiply_reduce_fusion
  193.6 5.8 fusion.60
  199.5 25.2 %fusion.63 = (f32[1024]{0:T(1024)S(1)}, bf16[2048,1024]{1,0:T(8,128)(2,1)}, f32[2048,1024]{1,0:T(8,128)}) fusion(f32[2048,1024]{1,0:T(8,128)S(1)} %fusion.60, f32[1024]{0:T(1024)S(1)} %copy-done.43, bf16[2048,1024]{1,0:T(8,128)(2,1)S(1)} %copy-done.22, bf16[1024,1024]{1,0:T(8,128)(2,1)S(1)} %copy-done), kind=kOutput, calls=%fused_computation.155 | convolution fusion | flops 4450155520 | bytes 27271168 | tf_op jit(solution)/shard_map/td,fd->tf/dot_general | solution.py:271
  224.7 10.1 %multiply_convert_fusion = bf16[2048,1024]{1,0:T(8,128)(2,1)} fusion(f32[2048,1024]{1,0:T(8,128)} %get-tuple-element.105, f32[2048,1024]{1,0:T(8,128)} %copy-done.21, f32[1024]{0:T(1024)S(1)} %copy-done.43), kind=kLoop, calls=%fused_computation.37 | loop fusion | flops 8388608 | bytes 20975616 | tf_op jit(solution)/shard_map/convert_element_type | solution.py:263
  234.7 7.1 convolution_convert_fusion.1
  241.9 2.0 copy-done.25
  246.8 5.8 convolution_convert_fusion.5
  252.6 3.9 copy.96
  256.6 7.4 convolution_convert_fusion.2
  266.2 2.6 add_convert_fusion.5
  270.6 2.4 add_convert_fusion.7
  273.2 44.1 %collective-permute-done.7 = bf16[1024,1024]{1,0:T(8,128)(2,1)S(1)} collective-permute-done((bf16[1024,1024]{1,0:T(8,128)(2,1)S(1)}, bf16[1024,1024]{1,0:T(8,128)(2,1)S(1)}, u32[]{:S(2)}, u32[]{:S(2)}) %collective-permute-start.7) | collective-permute-done | bytes 2097184 | tf_op jit(solution)/shard_map/ppermute | solution.py:199
  317.3 2.3 add_convert_fusion.4
  319.7 7.5 %fusion.35 = bf16[1024,1024]{1,0:T(8,128)(2,1)} fusion(bf16[2048,1024]{1,0:T(8,128)(2,1)S(1)} %copy-done.47, f32[1024]{0:T(1024)S(1)} %copy-done.46, f32[1024]{0:T(1024)S(1)} %copy-done.40, f32[2048]{0:T(1024)S(1)} %fusion.54, bf16[2048,1024]{1,0:T(8,128)(2,1)S(1)} %copy-done.7, f32[2048]{0:T(1024)S(1)} %broadcast_multiply_fusion, f32[1024]{0:T(1024)S(1)} %copy-done.33, ...), kind=kOutput, calls=%fused_computation.98 | convolution fusion | flops 4321181696 | bytes 14708736 | tf_op jit(solution)/shard_map/td,tf->df/dot_general | solution.py:275
  327.4 34.2 %collective-permute-done.4 = bf16[1024,1024]{1,0:T(8,128)(2,1)} collective-permute-done((bf16[1024,1024]{1,0:T(8,128)(2,1)}, bf16[1024,1024]{1,0:T(8,128)(2,1)}, u32[]{:S(2)}, u32[]{:S(2)}) %collective-permute-start.4) | collective-permute-done | bytes 2097184 | tf_op jit(solution)/shard_map/ppermute | solution.py:199
  361.6 3.2 add_convert_fusion.6
  364.9 2.6 broadcast_select_fusion.3
  369.6 6.3 fusion.10
  375.9 8.7 %fusion.15 = (f32[1024]{0:T(1024)S(1)}, f32[2048]{0:T(1024)S(1)}, f32[1024]{0:T(1024)S(1)}) fusion(f32[2048]{0:T(1024)S(1)} %fusion.54, bf16[1024,1024]{1,0:T(8,128)(2,1)S(1)} %get-tuple-element.113, bf16[1024,1024]{1,0:T(8,128)(2,1)S(1)} %get-tuple-element.112, f32[2048]{0:T(1024)S(1)} %broadcast_multiply_fusion, f32[1024]{0:T(1024)S(1)} %copy-done.33, ...), kind=kLoop, calls=%fused_computation.31 | loop fusion | flops 46133248 | bytes 12632064 | tf_op jit(solution)/shard_map/transpose(jvp())/reduce_sum | solution.py:176
  385.4 12.2 %fusion.65 = (f32[1024]{0:T(1024)S(1)}, f32[2048,1024]{1,0:T(8,128)S(1)}, bf16[2048,1024]{1,0:T(8,128)(2,1)}, f32[1024]{0:T(1024)S(1)}) fusion(f32[2048]{0:T(1024)S(1)} %negate_multiply_fusion.2, f32[2048]{0:T(1024)S(1)} %multiply_multiply_fusion.6, f32[2048]{0:T(1024)S(1)} %broadcast_multiply_fusion, f32[1024]{0:T(1024)S(1)} %copy-done.33, ...), kind=kLoop, calls=%fused_computation.156 | loop fusion | flops 60815360 | bytes 33607680 | tf_op jit(solution)/shard_map/reduce_sum | solution.py:284
  397.6 2.7 convolution_convert_fusion.3
  401.3 2.8 copy.81
  407.3 82.1 %segment_flash_bwd.1 = (f32[4,2048,64]{2,1,0:T(8,128)}, f32[4,2048,64]{2,1,0:T(8,128)}, f32[4,2048,64]{2,1,0:T(8,128)}) custom-call(s32[8]{0:T(128)S(1)} %fusion.56.lo_ref, s32[8]{0:T(128)S(1)} %fusion.55.hi_ref, s32[2048,1]{1,0:T(8,128)S(1)} %copy.79.segc_ref, s32[1,2048]{1,0:T(1,128)S(1)} %bitcast.87, bf16[4,2048,64]{2,1,0:T(8,128)(2,1)S(1)} %bitcast.81, ...), custom_call_target="tpu_custom_call" | custom-call | flops 6442450944 | bytes 12615680 | tf_op jit(solution)/shard_map/segment_flash_bwd/pallas_call | solution.py:154
  489.4 3.8 convert_bitcast_fusion
  493.1 1.9 copy.84
  496.4 3.8 bitcast_convert_fusion.2
  503.4 3.8 bitcast_convert_fusion.1
  510.6 5.8 bitcast_convert_fusion
  516.7 4.1 collective-permute-done.9
  520.8 2.3 add_convert_fusion.3
  524.9 4.7 fusion.44
  530.6 7.8 %fusion.41 = bf16[3,1024,256]{1,2,0:T(8,128)(2,1)} fusion(bf16[2048,1024]{1,0:T(8,128)(2,1)} %copy-done.24, bf16[1,2048,256]{2,1,0:T(8,128)(2,1)} %copy.88, bf16[1,2048,256]{2,1,0:T(8,128)(2,1)} %copy.87, bf16[1,2048,256]{2,1,0:T(8,128)(2,1)} %copy.86), kind=kOutput, calls=%fused_computation.101 | convolution fusion | flops 3225157632 | bytes 8912896 | tf_op jit(solution)/shard_map/td,stc->sdc/dot_general | solution.py:299
  538.5 4.4 copy.92
  542.9 3.1 copy.98
  546.0 25.1 %collective-permute-done.10 = bf16[1024,1024]{1,0:T(8,128)(2,1)} collective-permute-done((bf16[1024,1024]{1,0:T(8,128)(2,1)}, bf16[1024,1024]{1,0:T(8,128)(2,1)}, u32[]{:S(2)}, u32[]{:S(2)}) %collective-permute-start.10) | collective-permute-done | bytes 2097184 | tf_op jit(solution)/shard_map/ppermute | solution.py:199
  571.1 4.5 add_convert_fusion.2
  579.4 2.5 bitcast_reduce_fusion.1
  581.9 2.5 bitcast_reduce_fusion
  584.5 14.3 %reduce-scatter.15.cloned.1.call-done = bf16[128,256]{1,0:T(8,128)(2,1)} async-done(((bf16[1024,256]{1,0:T(8,128)(2,1)}), bf16[128,256]{1,0:T(8,128)(2,1)}) %reduce-scatter.15.cloned.1.call-update) | async-done | bytes 65552
  600.4 66.2 %reduce-scatter.13.cloned.1.call-done = bf16[128,768]{1,0:T(8,128)(2,1)} async-done(((bf16[1024,768]{1,0:T(8,128)(2,1)}), bf16[128,768]{1,0:T(8,128)(2,1)}) %reduce-scatter.13.cloned.1.call-update) | async-done | bytes 196624
  668.8 2.6 broadcast_select_fusion.1
  672.3 3.2 fusion.12
  675.5 7.0 fusion.16
  682.6 34.8 %psum.7 = f32[7680]{0:T(1024)S(1)} all-reduce(f32[7680]{0:T(1024)S(1)} %constant_dynamic-update-slice_fusion), channel_id=1, replica_groups=mesh['dp'=8,'mp'=4] {'dp'}, use_global_device_ids=true, to_apply=%region_20.22 | all-reduce | flops 7680 | bytes 61440 | tf_op jit(solution)/shard_map/psum | solution.py:329
  718.0 12.1 %add_add_fusion.2 = f32[2048,1024]{1,0:T(8,128)} fusion(f32[2048,1024]{1,0:T(8,128)} %copy-done.10, bf16[2048,1024]{1,0:T(8,128)(2,1)} %param.17, f32[2048]{0:T(1024)S(1)} %negate_multiply_fusion.1, f32[2048]{0:T(1024)S(1)} %multiply_multiply_fusion.5, f32[1024]{0:T(1024)S(1)} %copy-done.39, f32[2048]{0:T(1024)S(1)} %copy-done.32, f32[2048]{0:T(1024)S(1)} %copy-done.30, ...), kind=kLoop, calls=%fused_computation.34 | loop fusion | flops 27262976 | bytes 25202688 | tf_op jit(solution)/shard_map/add | solution.py:307
  (178 shorter events, 49.1 us)
Async XLA Ops:
  7.2 192.2 %copy-start = (bf16[1024,1024]{1,0:T(8,128)(2,1)S(1)}, bf16[1024,1024]{1,0:T(8,128)(2,1)}, u32[]{:S(2)}) copy-start(bf16[1024,1024]{1,0:T(8,128)(2,1)} %param.26) | copy-start | bytes 6291460
  7.2 568.4 %reduce-scatter.17.cloned.1.call-start = ((), (), s32[]{:S(2)}) async-start(), calls=%async_computation.7 | async-start | bytes 2359296
  11.3 3.5 copy-start.5
  11.3 5.8 copy-start.38
  11.3 5.8 copy-start.41
  14.7 5.8 copy-start.29
  16.1 0.6 copy-start.34
  16.7 3.8 copy-start.31
  17.1 3.4 copy-start.45
  20.5 4.6 copy-start.24
  35.7 1.6 copy-start.1
  111.6 1.3 copy-start.4
  118.2 2.0 copy-start.19
  121.7 4.6 collective-permute-start
  129.5 48.9 %collective-permute-start.1 = (bf16[1024,1024]{1,0:T(8,128)(2,1)S(1)}, bf16[1024,1024]{1,0:T(8,128)(2,1)S(1)}, u32[]{:S(2)}, u32[]{:S(2)}) collective-permute-start(bf16[1024,1024]{1,0:T(8,128)(2,1)S(1)} %add_convert_fusion.9), channel_id=1, source_target_pairs={{0,2},{1,3},{2,0},{3,1},{4,6},{5,7},{6,4},{7,5},{8,10},{9,11},{10,... | collective-permute-start | bytes 6291464 | tf_op jit(solution)/shard_map/ppermute | solution.py:199
  180.7 4.5 collective-permute-start.2
  180.7 7.0 copy-start.6
  180.8 7.0 copy-start.33
  187.7 5.8 copy-start.11
  187.8 5.8 copy-start.14
  189.4 4.2 copy-start.40
  189.4 4.2 copy-start.44
  189.4 4.2 copy-start.46
  192.9 0.6 copy-start.36
  193.6 5.9 copy-start.22
  193.6 5.9 copy-start.43
  199.4 25.2 %copy-start.21 = (f32[2048,1024]{1,0:T(8,128)}, f32[2048,1024]{1,0:T(8,128)S(1)}, u32[]{:S(2)}) copy-start(f32[2048,1024]{1,0:T(8,128)S(1)} %fusion.60) | copy-start | bytes 25165828
  234.7 10.8 %copy-start.27 = (bf16[2048,1024]{1,0:T(8,128)(2,1)S(1)}, bf16[2048,1024]{1,0:T(8,128)(2,1)}, u32[]{:S(2)}) copy-start(bf16[2048,1024]{1,0:T(8,128)(2,1)} %multiply_convert_fusion) | copy-start | bytes 12582916
  241.9 2.0 copy-start.25
  243.9 2.9 copy-start.23
  245.4 19.0 %collective-permute-start.6 = (bf16[1024,1024]{1,0:T(8,128)(2,1)}, bf16[1024,1024]{1,0:T(8,128)(2,1)}, u32[]{:S(2)}, u32[]{:S(2)}) collective-permute-start(bf16[1024,1024]{1,0:T(8,128)(2,1)} %constant_dynamic-slice_fusion.1), channel_id=1, source_target_pairs={{0,1},{1,0},{2,3},{3,2},{4,5},{5,4},{6,7},{7,6},{8,9},{9,8},{10,11... | collective-permute-start | bytes 6291464 | tf_op jit(solution)/shard_map/ppermute | solution.py:197
  256.6 321.0 %reduce-scatter.11.cloned.1.call-start = ((), (), s32[]{:S(2)}) async-start(), calls=%async_computation.4 | async-start | bytes 2359296 | tf_op jit(solution)/shard_map/reduce_scatter | solution.py:309
  264.0 2.2 copy-start.26
  264.2 6.4 collective-permute-start.3
  268.8 48.6 %collective-permute-start.7 = (bf16[1024,1024]{1,0:T(8,128)(2,1)S(1)}, bf16[1024,1024]{1,0:T(8,128)(2,1)S(1)}, u32[]{:S(2)}, u32[]{:S(2)}) collective-permute-start(bf16[1024,1024]{1,0:T(8,128)(2,1)S(1)} %add_convert_fusion.5), channel_id=1, source_target_pairs={{0,2},{1,3},{2,0},{3,1},{4,6},{5,7},{6,4},{7,5},{8,10},{9,11},{10,... | collective-permute-start | bytes 6291464 | tf_op jit(solution)/shard_map/ppermute | solution.py:199
  270.6 49.1 %copy-start.15 = (bf16[1024,1024]{1,0:T(8,128)(2,1)S(1)}, bf16[1024,1024]{1,0:T(8,128)(2,1)}, u32[]{:S(2)}) copy-start(bf16[1024,1024]{1,0:T(8,128)(2,1)} %copy-done.14) | copy-start | bytes 6291460
  270.6 49.1 %copy-start.47 = (bf16[2048,1024]{1,0:T(8,128)(2,1)S(1)}, bf16[2048,1024]{1,0:T(8,128)(2,1)}, u32[]{:S(2)}) copy-start(bf16[2048,1024]{1,0:T(8,128)(2,1)} %get-tuple-element.104) | copy-start | bytes 12582916
  272.9 46.7 %copy-start.7 = (bf16[2048,1024]{1,0:T(8,128)(2,1)S(1)}, bf16[2048,1024]{1,0:T(8,128)(2,1)}, u32[]{:S(2)}) copy-start(bf16[2048,1024]{1,0:T(8,128)(2,1)} %param.17) | copy-start | bytes 12582916
  272.9 46.7 %copy-start.12 = (bf16[1024,1024]{1,0:T(8,128)(2,1)S(1)}, bf16[1024,1024]{1,0:T(8,128)(2,1)}, u32[]{:S(2)}) copy-start(bf16[1024,1024]{1,0:T(8,128)(2,1)} %copy-done.11) | copy-start | bytes 6291460
  272.9 88.6 %collective-permute-start.4 = (bf16[1024,1024]{1,0:T(8,128)(2,1)}, bf16[1024,1024]{1,0:T(8,128)(2,1)}, u32[]{:S(2)}, u32[]{:S(2)}) collective-permute-start(bf16[1024,1024]{1,0:T(8,128)(2,1)} %add_convert_fusion.7), channel_id=1, source_target_pairs={{0,2},{1,3},{2,0},{3,1},{4,6},{5,7},{6,4},{7,5},{8,10},{9,11},{10,... | collective-permute-start | bytes 6291464 | tf_op jit(solution)/shard_map/ppermute | solution.py:199
  319.7 45.3 %collective-permute-start.8 = (bf16[1024,1024]{1,0:T(8,128)(2,1)}, bf16[1024,1024]{1,0:T(8,128)(2,1)}, u32[]{:S(2)}, u32[]{:S(2)}) collective-permute-start(bf16[1024,1024]{1,0:T(8,128)(2,1)} %add_convert_fusion.4), channel_id=1, source_target_pairs={{0,1},{1,0},{2,3},{3,2},{4,5},{5,4},{6,7},{7,6},{8,9},{9,8},{10,11... | collective-permute-start | bytes 6291464 | tf_op jit(solution)/shard_map/ppermute | solution.py:201
  327.2 271.6 %reduce-scatter.15.cloned.1.call-start = ((), (), s32[]{:S(2)}) async-start(), calls=%async_computation.6 | async-start | bytes 589824
  364.8 3.5 copy-start.8
  364.8 4.1 copy-start.13
  364.8 4.8 copy-start.16
  364.9 19.9 %collective-permute-start.5 = (bf16[1024,1024]{1,0:T(8,128)(2,1)S(1)}, bf16[1024,1024]{1,0:T(8,128)(2,1)S(1)}, u32[]{:S(2)}, u32[]{:S(2)}) collective-permute-start(bf16[1024,1024]{1,0:T(8,128)(2,1)S(1)} %add_convert_fusion.6), channel_id=1, source_target_pairs={{0,1},{1,0},{2,3},{3,2},{4,5},{5,4},{6,7},{7,6},{8,9},{9,8},{10,11... | collective-permute-start | bytes 6291464 | tf_op jit(solution)/shard_map/ppermute | solution.py:201
  369.6 6.3 copy-start.37
  384.7 0.7 copy-start.42
  385.4 12.2 %copy-start.28 = (bf16[256,1024]{1,0:T(8,128)(2,1)S(1)}, bf16[256,1024]{1,0:T(8,128)(2,1)}, u32[]{:S(2)}) copy-start(bf16[256,1024]{1,0:T(8,128)(2,1)} %param.22) | copy-start | bytes 1572868
  397.6 3.7 copy-start.10
  404.1 1.6 copy-start.2
  405.7 1.6 copy-start.3
  516.6 8.2 %copy-start.20 = (bf16[2048,4,64]{0,2,1:T(8,128)(2,1)S(1)}, bf16[2048,4,64]{0,2,1:T(8,128)(2,1)}, u32[]{:S(2)}) copy-start(bf16[2048,4,64]{0,2,1:T(8,128)(2,1)} %copy.80) | copy-start | bytes 3145732
  516.6 4.2 collective-permute-start.9
  523.1 48.0 %collective-permute-start.10 = (bf16[1024,1024]{1,0:T(8,128)(2,1)}, bf16[1024,1024]{1,0:T(8,128)(2,1)}, u32[]{:S(2)}, u32[]{:S(2)}) collective-permute-start(bf16[1024,1024]{1,0:T(8,128)(2,1)} %add_convert_fusion.3), channel_id=1, source_target_pairs={{0,2},{1,3},{2,0},{3,1},{4,6},{5,7},{6,4},{7,5},{8,10},{9,11},{10,... | collective-permute-start | bytes 6291464 | tf_op jit(solution)/shard_map/ppermute | solution.py:199
  530.6 136.1 %reduce-scatter.13.cloned.1.call-start = ((), (), s32[]{:S(2)}) async-start(), calls=%async_computation.5 | async-start | bytes 1769472
  575.6 93.2 %collective-permute-start.11 = (bf16[1024,1024]{1,0:T(8,128)(2,1)}, bf16[1024,1024]{1,0:T(8,128)(2,1)}, u32[]{:S(2)}, u32[]{:S(2)}) collective-permute-start(bf16[1024,1024]{1,0:T(8,128)(2,1)} %add_convert_fusion.2), channel_id=1, source_target_pairs={{0,1},{1,0},{2,3},{3,2},{4,5},{5,4},{6,7},{7,6},{8,9},{9,8},{10,11... | collective-permute-start | bytes 6291464 | tf_op jit(solution)/shard_map/ppermute | solution.py:201
  668.8 3.4 copy-start.9
  668.8 3.4 copy-start.30
  668.8 3.5 copy-start.39
  671.5 4.0 copy-start.17
  671.5 4.0 copy-start.18
  672.2 3.2 copy-start.35
  672.2 3.2 copy-start.32
Sparse Core Ops, SparseCore 0:
  256.7 70.8 reduce-scatter.16
  331.1 67.4 reduce-scatter.10
  530.7 68.0 reduce-scatter.14
  602.1 64.5 reduce-scatter.12
